TPU v7x, 512 devices: a 8x2x16 block of a 8x8x16 slice. The times are simulated.
512 devices in a mesh: sweep: 2 (over y), tm: 128 (over x, z), unit: 2 (over core).
Axes of the slice: x: 8, y: 2, z: 16, core: 2. Of those that a mesh axis runs over, the one named last changes fastest.
The devices are a block of a 8x8x16 slice.
Arguments:
- projections: bfloat16 [2, 512, 3, 1024], P('sweep', 'tm', None, 'unit'), parts along dimension 0, may hold values from -6 to 6
- recurrent: bfloat16 [2048, 3, 1024], P('sweep', None, 'unit'), parts along dimension 0, may hold values from -0.375 to 0.375
- update_bias: float32 [2048], P(('sweep', 'unit')), parts along dimension 0, may hold values from -1 to 13
- candidate_bias: float32 [2048], P(('sweep', 'unit')), parts along dimension 0, may hold values from -5 to 5
- start_state: float32 [2, 1024], P('sweep', 'unit'), parts along dimension 0, may hold values from -4 to 4
- initial_guess: float32 [2, 512, 1024], P('sweep', 'tm', 'unit'), parts along dimension 0, may hold values from -3 to 3
Outputs:
- trajectory: float32 [2, 512, 1024], P('sweep', 'tm', 'unit'), parts along dimension 0
There are 2 independent parts, one for each index of `sweep`. A program takes and returns all parts, laid end to end along the dimension named above; each array names one. Nothing has to cross between parts.
All inputs are finite; a program needn't handle non-finite values.
Results may differ from a plain program's by a relative error of at most 0.0017.
Values may be sent and summed in bfloat16 or wider, within the bound.
No kernel may reach another device: no remote copies, remote signals or barrier semaphores. Data moves between devices by JAX's collectives and lax.ppermute only.
A program may use at most 64 MiB of HBM per device.

v0:
```python
import jax
import jax.numpy as jnp
from jax import lax
from jax.sharding import Mesh
from jax.sharding import PartitionSpec as P

BLOCK = 128
NEWTON = 2
TM = ("tm_0", "tm_1")


HIGHEST_MODE = lax.Precision.HIGHEST


def passed_along(value, axis, steps):
    count = lax.axis_size(axis)
    initial, last = (max(0, -steps), min(count, count - steps))
    return lax.ppermute(value, axis, [(source, source + steps) for source in range(initial, last)])


def copy_for_each(value, axis):
    copies = jnp.broadcast_to(value, (lax.axis_size(axis), *value.shape))
    return lax.all_to_all(copies, axis, split_axis=0, concat_axis=0, tiled=True)


def in_order(tiles, dim):
    tiles = jnp.moveaxis(tiles, 0, dim)
    shape = tiles.shape
    return tiles.reshape(*shape[:dim], shape[dim] * shape[dim + 1], *shape[dim + 2 :])


def collect(value, axis, dim):
    tiles = copy_for_each(value, axis)
    return in_order(tiles, dim)


def filled_with(value, identity):
    return jax.tree.map(
        lambda part, zero: jnp.zeros_like(part) + jnp.asarray(zero, part.dtype), value, identity
    )


def carried_in(value, axes, combine, identity):
    before = start = filled_with(value, identity)
    running = value
    for axis in reversed(axes):
        length, here = (lax.axis_size(axis), lax.axis_index(axis))
        pieces = jax.tree.map(lambda part: lax.all_gather(part, axis), running)
        inside, running = (start, start)
        for k in range(length):
            passed = k < here
            running = combine(running, jax.tree.map(lambda part: part[k], pieces))
            inside = jax.tree.map(lambda new, old: jnp.where(passed, new, old), running, inside)
        before = combine(inside, before)
    return before


def combine(earlier, later):
    matrix = jnp.einsum("pji,pik->pjk", later[0], earlier[0], precision=HIGHEST_MODE)
    vector = jnp.einsum("pji,pi->pj", later[0], earlier[1], precision=HIGHEST_MODE) + later[1]
    return (matrix, vector)


def apply_map(matrix, vector, current):
    return jnp.einsum("pji,pi->pj", matrix, current, precision=HIGHEST_MODE) + vector


def advance_keep(current, inputs):
    following = apply_map(inputs[0], inputs[1], current)
    return (following, following)


def advance_last(current, inputs):
    return (apply_map(inputs[0], inputs[1], current), None)


def compose(product, jac_step):
    return (jnp.einsum("pji,pik->pjk", jac_step, product, precision=HIGHEST_MODE), None)


def to_time(values, num_blocks):
    moved = jnp.transpose(values, (1, 0, 2))
    return moved.reshape(moved.shape[0], moved.shape[1], num_blocks, BLOCK)


def shards(projections, recurrent, update_bias, candidate_bias, start_state, initial_guess):
    num_batch, num_steps, _, width_dev = projections.shape
    full_width = recurrent.shape[0]
    num_blocks = width_dev // BLOCK
    num_pairs = num_batch * num_blocks
    unit_place = lax.axis_index("unit")
    time_place = lax.axis_index(TM)
    flat_weight = recurrent.reshape(full_width, 3 * width_dev)
    own_rows = lax.dynamic_slice_in_dim(recurrent, unit_place * width_dev, width_dev, 0)
    own_rows = own_rows.astype(jnp.float32).reshape(num_blocks, BLOCK, 3, num_blocks, BLOCK)
    diagonal = jnp.einsum("kigkj->gkji", own_rows)
    identity = jnp.eye(BLOCK, dtype=jnp.float32)
    start_pairs = start_state.reshape(num_pairs, BLOCK)
    last_guess = passed_along(initial_guess[:, -1, :], TM, 1)
    entering = jnp.where(time_place == 0, start_state, last_guess)
    trajectory = initial_guess
    for newton_turn in range(NEWTON):
        previous = jnp.concatenate([entering[:, None, :], trajectory[:, :-1, :]], axis=1)
        panels = previous.astype(jnp.bfloat16).reshape(num_batch * num_steps, width_dev)
        recurrent_terms = jnp.dot(
            collect(panels, "unit", 1), flat_weight, preferred_element_type=jnp.float32
        )
        recurrent_terms = recurrent_terms.reshape(num_batch, num_steps, 3, width_dev)
        update_gate = jax.nn.sigmoid(
            projections[:, :, 0].astype(jnp.float32) + recurrent_terms[:, :, 0] + update_bias
        )
        reset_gate = jax.nn.sigmoid(
            projections[:, :, 1].astype(jnp.float32) + recurrent_terms[:, :, 1]
        )
        cand_rec = recurrent_terms[:, :, 2] + candidate_bias
        candidate = jnp.tanh(projections[:, :, 2].astype(jnp.float32) + reset_gate * cand_rec)
        mapped = (1.0 - update_gate) * candidate + update_gate * previous
        coef_a = to_time((previous - candidate) * update_gate * (1.0 - update_gate), num_blocks)
        coef_full = (1.0 - update_gate) * (1.0 - candidate * candidate) * reset_gate
        coef_c = to_time(coef_full * cand_rec * (1.0 - reset_gate), num_blocks)
        coef_d = to_time(coef_full, num_blocks)
        gate_time = to_time(update_gate, num_blocks)
        jacobian = (
            coef_a[..., None] * diagonal[0]
            + coef_c[..., None] * diagonal[1]
            + coef_d[..., None] * diagonal[2]
            + gate_time[..., None] * identity
        )
        jacobian = jacobian.reshape(num_steps, num_pairs, BLOCK, BLOCK)
        prev_pairs = to_time(previous, num_blocks).reshape(num_steps, num_pairs, BLOCK)
        mapped_pairs = to_time(mapped, num_blocks).reshape(num_steps, num_pairs, BLOCK)
        offsets = mapped_pairs - jnp.einsum(
            "tpji,tpi->tpj", jacobian, prev_pairs, precision=HIGHEST_MODE
        )
        stretch_matrix, _ = lax.scan(compose, jacobian[0], jacobian[1:])
        stretch_vector, _ = lax.scan(
            advance_last, jnp.zeros((num_pairs, BLOCK), jnp.float32), (jacobian, offsets)
        )
        neutral = (
            jnp.broadcast_to(identity, (num_pairs, BLOCK, BLOCK)),
            jnp.zeros((num_pairs, BLOCK), jnp.float32),
        )
        prefix_matrix, prefix_vector = carried_in(
            (stretch_matrix, stretch_vector), TM, combine, neutral
        )
        entering_pairs = apply_map(prefix_matrix, prefix_vector, start_pairs)
        carried, states = lax.scan(advance_keep, entering_pairs, (jacobian, offsets))
        trajectory = jnp.transpose(states.reshape(num_steps, num_batch, width_dev), (1, 0, 2))
        entering = entering_pairs.reshape(num_batch, width_dev)
    return trajectory


def solution(mesh):
    finer = Mesh(
        mesh.devices.reshape(mesh.shape["sweep"], 8, 16, mesh.shape["unit"]),
        ("sweep", "tm_0", "tm_1", "unit"),
    )
    return jax.shard_map(
        shards,
        mesh=finer,
        in_specs=(
            P("sweep", TM, None, "unit"),
            P("sweep", None, "unit"),
            P(("sweep", "unit")),
            P(("sweep", "unit")),
            P("sweep", "unit"),
            P("sweep", TM, "unit"),
        ),
        out_specs=P("sweep", TM, "unit"),
        check_vma=False,
    )
```

profile of v0, /device:TPU:80, one launch (start us, length us, event | category | flops | bytes accessed | tf_op | source)
XLA Modules:
  0.0 458.5 jit_solution(9501292064284692435)
XLA Ops:
  7.3 6.0 %collective-permute-start = (f32[1,512]{1,0:T(1,128)S(1)}, f32[1,512]{1,0:T(1,128)S(1)}, u32[]{:S(2)}, u32[]{:S(2)}) collective-permute-start(f32[1,512]{1,0:T(1,128)S(1)} %slice_bitcast_fusion.55), channel_id=1, source_target_pairs={{0,2},{2,4},{4,6},{6,8},{8,10},{10,12},{12,14},{14,16},{16,18},{18... | collective-permute-start | bytes 6152 | tf_op jit(solution)/shard_map/ppermute | solution.py:18
  14.7 3.5 dynamic-slice_convert_fusion
  18.2 3.1 reshape.762
  23.2 3.2 copy.8
  27.5 1.9 copy.10
  29.5 1.8 copy.9
  31.3 3.7 all_to_all.10
  37.5 2.2 multiply_add_fusion.3
  40.6 4.2 while.66
  45.7 2.3 multiply_add_fusion.2
  48.0 1.7 fusion.181
  49.8 6.0 %while.70 = (s32[]{:T(128)}, f32[4,128]{1,0:T(4,128)S(1)}, f32[4,4,128,128]{3,2,1,0:T(8,128)}, f32[4,4,128]{2,1,0:T(4,128)S(1)}, s32[]{:T(128)}, /*index=5*/s32[]{:T(128)}) while((s32[]{:T(128)}, f32[4,128]{1,0:T(4,128)S(1)}, f32[4,4,128,128]{3,2,1,0:T(8,128)}, f32[4,4,128]{2,1,0:T(4,128)S(1)}, s32[]{:T(128)}, ...), condition=%wide.region_4.5_spmd.clone, body=%wide.region_3.4_spmd.clone.sunk | while | flops 787459 | bytes 276575 | solution.py:136
  49.8 1.5 fusion.520
  51.3 1.5 fusion.520
  52.8 1.5 fusion.520
  54.3 1.5 fusion.520
  55.8 66.7 %all-gather.8 = f32[16,4,128]{2,1,0:T(4,128)} all-gather(f32[1,4,128]{2,1,0:T(4,128)S(1)} %bitcast.879), channel_id=4, replica_groups=mesh['sweep'=2,'tm_0'=8,'tm_1'=16,'unit'=2] {'tm_1'}, dimensions={0}, use_global_device_ids=true | all-gather | bytes 34816 | tf_op jit(solution)/shard_map/all_gather | solution.py:48
  122.4 33.4 %all-gather.17.cloned.1.call-done = f32[64,128,128]{2,1,0:T(8,128)} async-done(((f32[4,128,128]{2,1,0:T(8,128)}), f32[64,128,128]{2,1,0:T(8,128)}) %all-gather.17.cloned.1.call-update) | async-done | bytes 4194320 | tf_op jit(solution)/shard_map/all_gather | solution.py:48
  155.8 1.5 fusion.80
  169.0 1.5 fusion.208
  180.0 1.7 fusion.213
  188.8 1.5 fusion.217
  193.1 1.5 fusion.219
  197.4 1.5 fusion.221
  203.8 25.9 %all-gather.9 = f32[8,4,128]{2,1,0:T(4,128)} all-gather(f32[1,4,128]{2,1,0:T(4,128)S(1)} %fusion.177), channel_id=5, replica_groups=mesh['sweep'=2,'tm_0'=8,'tm_1'=16,'unit'=2] {'tm_0'}, dimensions={0}, use_global_device_ids=true | all-gather | bytes 18432 | tf_op jit(solution)/shard_map/all_gather | solution.py:48
  232.2 1.5 fusion.77
  257.2 6.0 %while.67 = (s32[]{:T(128)}, f32[4,128]{1,0:T(4,128)S(1)}, f32[4,4,128]{2,1,0:T(4,128)S(1)}, f32[4,4,128,128]{3,2,1,0:T(8,128)}, f32[4,4,128]{2,1,0:T(4,128)S(1)}, /*index=5*/s32[]{:T(128)}) while((s32[]{:T(128)}, f32[4,128]{1,0:T(4,128)S(1)}, f32[4,4,128]{2,1,0:T(4,128)S(1)}, f32[4,4,128,128]{3,2,1,0:T(8,128)}, f32[4,4,128]{2,1,0:T(4,128)S(1)}, ...), condition=%wide.region_6.7_spmd, body=%wide.region_5.6_spmd.sunk | while | flops 786946 | bytes 274517 | solution.py:147
  257.2 1.5 fusion.511
  258.7 1.5 fusion.511
  260.2 1.5 fusion.511
  261.7 1.5 fusion.511
  263.2 3.7 all_to_all.11
  268.0 2.2 multiply_add_fusion.1
  273.9 1.7 fusion.184
  275.6 2.2 while.71
  277.8 30.4 %all-gather.10 = f32[16,4,128]{2,1,0:T(4,128)} all-gather(f32[1,4,128]{2,1,0:T(4,128)S(1)} %bitcast.880), channel_id=8, replica_groups=mesh['sweep'=2,'tm_0'=8,'tm_1'=16,'unit'=2] {'tm_1'}, dimensions={0}, use_global_device_ids=true | all-gather | bytes 34816 | tf_op jit(solution)/shard_map/all_gather | solution.py:48
  308.3 37.5 %all-gather.21.cloned.1.call-done = f32[64,128,128]{2,1,0:T(8,128)} async-done(((f32[4,128,128]{2,1,0:T(8,128)}), f32[64,128,128]{2,1,0:T(8,128)}) %all-gather.21.cloned.1.call-update) | async-done | bytes 4194320 | tf_op jit(solution)/shard_map/all_gather | solution.py:48
  345.8 1.5 fusion.73
  361.2 1.5 fusion.253
  363.4 1.5 fusion.254
  378.6 1.5 fusion.261
  380.7 1.5 fusion.262
  387.2 1.5 fusion.265
  389.3 1.5 fusion.266
  393.6 1.5 fusion.268
  395.8 25.7 %all-gather.11 = f32[8,4,128]{2,1,0:T(4,128)} all-gather(f32[1,4,128]{2,1,0:T(4,128)S(1)} %fusion.178), channel_id=9, replica_groups=mesh['sweep'=2,'tm_0'=8,'tm_1'=16,'unit'=2] {'tm_0'}, dimensions={0}, use_global_device_ids=true | all-gather | bytes 18432 | tf_op jit(solution)/shard_map/all_gather | solution.py:48
  424.1 1.5 fusion.68
  448.9 2.2 while.69
  (375 shorter events, 152.6 us)
Async XLA Ops:
  6.5 149.3 %all-gather.17.cloned.1.call-start = ((), (), s32[]{:S(2)}) async-start(), calls=%async_computation.2 | async-start | bytes 4456448 | tf_op jit(solution)/shard_map/all_gather | solution.py:48
  7.3 24.0 %collective-permute-start = (f32[1,512]{1,0:T(1,128)S(1)}, f32[1,512]{1,0:T(1,128)S(1)}, u32[]{:S(2)}, u32[]{:S(2)}) collective-permute-start(f32[1,512]{1,0:T(1,128)S(1)} %slice_bitcast_fusion.55), channel_id=1, source_target_pairs={{0,2},{2,4},{4,6},{6,8},{8,10},{10,12},{12,14},{14,16},{16,18},{18... | collective-permute-start | bytes 6152 | tf_op jit(solution)/shard_map/ppermute | solution.py:18
  22.2 4.2 copy-start.59
  23.2 8.1 %copy-start.60 = (f32[1,512]{1,0:T(1,128)S(1)}, f32[1,512]{1,0:T(1,128)}, u32[]{:S(2)}) copy-start(f32[1,512]{1,0:T(1,128)} %param.22) | copy-start | bytes 6148
  23.2 12.8 %copy-start.55 = (bf16[1,4,3,512]{3,1,2,0:T(4,128)(2,1)S(1)}, bf16[1,4,3,512]{3,1,2,0:T(4,128)(2,1)}, u32[]{:S(2)}) copy-start(bf16[1,4,3,512]{3,1,2,0:T(4,128)(2,1)} %param.18) | copy-start | bytes 36868
  23.2 12.8 %copy-start.57 = (f32[512]{0:T(512)S(1)}, f32[512]{0:T(512)}, u32[]{:S(2)}) copy-start(f32[512]{0:T(512)} %param.21) | copy-start | bytes 6148
  27.5 9.9 %copy-start.7 = (f32[4,128,128]{2,1,0:T(8,128)}, f32[4,128,128]{2,1,0:T(8,128)S(1)}, u32[]{:S(2)}) copy-start(f32[4,128,128]{2,1,0:T(8,128)S(1)} %copy.11) | copy-start | bytes 786436
  31.3 5.5 %copy-start.62 = (f32[1,512]{1,0:T(1,128)}, f32[1,512]{1,0:T(1,128)S(1)}, u32[]{:S(2)}) copy-start(f32[1,512]{1,0:T(1,128)S(1)} %get-tuple-element.238) | copy-start | bytes 6148
  40.6 9.1 %copy-start.63 = (f32[1,512]{1,0:T(1,128)S(1)}, f32[1,512]{1,0:T(1,128)}, u32[]{:S(2)}) copy-start(f32[1,512]{1,0:T(1,128)} %copy-done.62) | copy-start | bytes 6148
  45.6 186.6 %all-gather.19.cloned.1.call-start = ((), (), s32[]{:S(2)}) async-start(), calls=%async_computation.3 | async-start | bytes 2359296 | tf_op jit(solution)/shard_map/all_gather | solution.py:48
  155.8 6.3 %copy-start = (f32[64,128,128]{2,1,0:T(8,128)S(1)}, f32[64,128,128]{2,1,0:T(8,128)}, u32[]{:S(2)}) copy-start(f32[64,128,128]{2,1,0:T(8,128)} %all-gather.17.cloned.1.call-done) | copy-start | bytes 12582916
  160.7 3.9 copy-start.21
  163.4 2.9 copy-start.29
  163.8 2.9 copy-start.31
  169.0 176.8 %all-gather.21.cloned.1.call-start = ((), (), s32[]{:S(2)}) async-start(), calls=%async_computation.4 | async-start | bytes 4456448 | tf_op jit(solution)/shard_map/all_gather | solution.py:48
  179.0 51.8 %copy-start.22 = (f32[4,128,128]{2,1,0:T(8,128)S(1)}, f32[4,128,128]{2,1,0:T(8,128)}, u32[]{:S(2)}) copy-start(f32[4,128,128]{2,1,0:T(8,128)} %copy-done.21) | copy-start | bytes 786436
  179.0 51.8 %copy-start.24 = (f32[4,128,128]{2,1,0:T(8,128)S(1)}, f32[4,128,128]{2,1,0:T(8,128)}, u32[]{:S(2)}) copy-start(f32[4,128,128]{2,1,0:T(8,128)} %copy-done.23) | copy-start | bytes 786436
  179.0 51.8 %copy-start.26 = (f32[4,128,128]{2,1,0:T(8,128)S(1)}, f32[4,128,128]{2,1,0:T(8,128)}, u32[]{:S(2)}) copy-start(f32[4,128,128]{2,1,0:T(8,128)} %copy-done.25) | copy-start | bytes 786436
  179.0 51.8 %copy-start.28 = (f32[4,128,128]{2,1,0:T(8,128)S(1)}, f32[4,128,128]{2,1,0:T(8,128)}, u32[]{:S(2)}) copy-start(f32[4,128,128]{2,1,0:T(8,128)} %copy-done.27) | copy-start | bytes 786436
  179.0 51.8 %copy-start.30 = (f32[4,128,128]{2,1,0:T(8,128)S(1)}, f32[4,128,128]{2,1,0:T(8,128)}, u32[]{:S(2)}) copy-start(f32[4,128,128]{2,1,0:T(8,128)} %copy-done.29) | copy-start | bytes 786436
  179.0 51.8 %copy-start.32 = (f32[4,128,128]{2,1,0:T(8,128)S(1)}, f32[4,128,128]{2,1,0:T(8,128)}, u32[]{:S(2)}) copy-start(f32[4,128,128]{2,1,0:T(8,128)} %copy-done.31) | copy-start | bytes 786436
  179.0 51.8 %copy-start.34 = (f32[4,128,128]{2,1,0:T(8,128)S(1)}, f32[4,128,128]{2,1,0:T(8,128)}, u32[]{:S(2)}) copy-start(f32[4,128,128]{2,1,0:T(8,128)} %copy-done.33) | copy-start | bytes 786436
  179.1 51.8 %copy-start.36 = (f32[4,128,128]{2,1,0:T(8,128)S(1)}, f32[4,128,128]{2,1,0:T(8,128)}, u32[]{:S(2)}) copy-start(f32[4,128,128]{2,1,0:T(8,128)} %copy-done.35) | copy-start | bytes 786436
  179.1 51.8 %copy-start.38 = (f32[4,128,128]{2,1,0:T(8,128)S(1)}, f32[4,128,128]{2,1,0:T(8,128)}, u32[]{:S(2)}) copy-start(f32[4,128,128]{2,1,0:T(8,128)} %copy-done.37) | copy-start | bytes 786436
  179.1 51.8 %copy-start.40 = (f32[4,128,128]{2,1,0:T(8,128)S(1)}, f32[4,128,128]{2,1,0:T(8,128)}, u32[]{:S(2)}) copy-start(f32[4,128,128]{2,1,0:T(8,128)} %copy-done.39) | copy-start | bytes 786436
  179.1 51.8 %copy-start.42 = (f32[4,128,128]{2,1,0:T(8,128)S(1)}, f32[4,128,128]{2,1,0:T(8,128)}, u32[]{:S(2)}) copy-start(f32[4,128,128]{2,1,0:T(8,128)} %copy-done.41) | copy-start | bytes 786436
  179.1 51.8 %copy-start.44 = (f32[4,128,128]{2,1,0:T(8,128)S(1)}, f32[4,128,128]{2,1,0:T(8,128)}, u32[]{:S(2)}) copy-start(f32[4,128,128]{2,1,0:T(8,128)} %copy-done.43) | copy-start | bytes 786436
  179.1 51.8 %copy-start.46 = (f32[4,128,128]{2,1,0:T(8,128)S(1)}, f32[4,128,128]{2,1,0:T(8,128)}, u32[]{:S(2)}) copy-start(f32[4,128,128]{2,1,0:T(8,128)} %copy-done.45) | copy-start | bytes 786436
  179.1 51.8 %copy-start.49 = (f32[4,128,128]{2,1,0:T(8,128)S(1)}, f32[4,128,128]{2,1,0:T(8,128)}, u32[]{:S(2)}) copy-start(f32[4,128,128]{2,1,0:T(8,128)} %fusion.200) | copy-start | bytes 786436
  179.1 51.8 %copy-start.54 = (f32[4,128,128]{2,1,0:T(8,128)S(1)}, f32[4,128,128]{2,1,0:T(8,128)}, u32[]{:S(2)}) copy-start(f32[4,128,128]{2,1,0:T(8,128)} %copy-done.53) | copy-start | bytes 786436
  232.2 5.6 %copy-start.3 = (f32[32,128,128]{2,1,0:T(8,128)S(1)}, f32[32,128,128]{2,1,0:T(8,128)}, u32[]{:S(2)}) copy-start(f32[32,128,128]{2,1,0:T(8,128)} %all-gather.19.cloned.1.call-done) | copy-start | bytes 6291460
  236.4 3.0 copy-start.50
  236.4 3.4 copy-start.61
  247.3 20.6 %copy-start.56 = (bf16[1,4,3,512]{3,1,2,0:T(4,128)(2,1)S(1)}, bf16[1,4,3,512]{3,1,2,0:T(4,128)(2,1)}, u32[]{:S(2)}) copy-start(bf16[1,4,3,512]{3,1,2,0:T(4,128)(2,1)} %param.18) | copy-start | bytes 36868
  247.3 20.7 %copy-start.58 = (f32[512]{0:T(512)S(1)}, f32[512]{0:T(512)}, u32[]{:S(2)}) copy-start(f32[512]{0:T(512)} %param.21) | copy-start | bytes 6148
  247.3 20.7 %copy-start.64 = (f32[512]{0:T(512)S(1)}, f32[512]{0:T(512)}, u32[]{:S(2)}) copy-start(f32[512]{0:T(512)} %param.20) | copy-start | bytes 6148
  247.3 20.7 %copy-start.8 = (f32[4,128,128]{2,1,0:T(8,128)S(1)}, f32[4,128,128]{2,1,0:T(8,128)}, u32[]{:S(2)}) copy-start(f32[4,128,128]{2,1,0:T(8,128)} %copy-done.7) | copy-start | bytes 786436
  272.5 151.6 %all-gather.23.cloned.1.call-start = ((), (), s32[]{:S(2)}) async-start(), calls=%async_computation.5 | async-start | bytes 2359296 | tf_op jit(solution)/shard_map/all_gather | solution.py:48
  345.8 6.2 %copy-start.1 = (f32[64,128,128]{2,1,0:T(8,128)S(1)}, f32[64,128,128]{2,1,0:T(8,128)}, u32[]{:S(2)}) copy-start(f32[64,128,128]{2,1,0:T(8,128)} %all-gather.21.cloned.1.call-done) | copy-start | bytes 12582916
  371.3 51.4 %copy-start.12 = (f32[4,128,128]{2,1,0:T(8,128)S(1)}, f32[4,128,128]{2,1,0:T(8,128)}, u32[]{:S(2)}) copy-start(f32[4,128,128]{2,1,0:T(8,128)} %copy-done.11) | copy-start | bytes 786436
  371.3 51.4 %copy-start.14 = (f32[4,128,128]{2,1,0:T(8,128)S(1)}, f32[4,128,128]{2,1,0:T(8,128)}, u32[]{:S(2)}) copy-start(f32[4,128,128]{2,1,0:T(8,128)} %copy-done.13) | copy-start | bytes 786436
  371.3 51.4 %copy-start.16 = (f32[4,128,128]{2,1,0:T(8,128)S(1)}, f32[4,128,128]{2,1,0:T(8,128)}, u32[]{:S(2)}) copy-start(f32[4,128,128]{2,1,0:T(8,128)} %copy-done.15) | copy-start | bytes 786436
  371.3 51.4 %copy-start.18 = (f32[4,128,128]{2,1,0:T(8,128)S(1)}, f32[4,128,128]{2,1,0:T(8,128)}, u32[]{:S(2)}) copy-start(f32[4,128,128]{2,1,0:T(8,128)} %copy-done.17) | copy-start | bytes 786436
  371.3 51.4 %copy-start.20 = (f32[4,128,128]{2,1,0:T(8,128)S(1)}, f32[4,128,128]{2,1,0:T(8,128)}, u32[]{:S(2)}) copy-start(f32[4,128,128]{2,1,0:T(8,128)} %copy-done.19) | copy-start | bytes 786436
  371.3 51.4 %copy-start.47 = (f32[4,128,128]{2,1,0:T(8,128)S(1)}, f32[4,128,128]{2,1,0:T(8,128)}, u32[]{:S(2)}) copy-start(f32[4,128,128]{2,1,0:T(8,128)} %fusion.245) | copy-start | bytes 786436
  371.3 51.4 %copy-start.52 = (f32[4,128,128]{2,1,0:T(8,128)S(1)}, f32[4,128,128]{2,1,0:T(8,128)}, u32[]{:S(2)}) copy-start(f32[4,128,128]{2,1,0:T(8,128)} %copy-done.51) | copy-start | bytes 786436
  424.1 5.6 %copy-start.2 = (f32[32,128,128]{2,1,0:T(8,128)S(1)}, f32[32,128,128]{2,1,0:T(8,128)}, u32[]{:S(2)}) copy-start(f32[32,128,128]{2,1,0:T(8,128)} %all-gather.23.cloned.1.call-done) | copy-start | bytes 6291460
  428.2 3.0 copy-start.48
  (22 other events, 31.9 us)
Sparse Core Ops, SparseCore 0:
  45.7 110.0 all-gather.16
  169.1 42.8 all-gather.18
  272.6 73.1 all-gather.20
  361.3 43.3 all-gather.22
where the time goes:
time: 468 us; the launch traced here: 458 us
  blocking collectives  156 us (33%)
  matrix products  137 us (29%)
  waiting for transfers between devices  71.1 us (15%)
  other arithmetic  49.4 us (11%)
  local copies, waits for them, and re-layouts  23.1 us (5%)
  between operations  14.9 us (3%)
  starting transfers between devices  6.38 us (1%)
    all_gather x4, blocking collectives, carried_in(): pieces = jax.tree.map(lambda part: lax.all_gather(part, axis), running)  149 us
    all_gather x4, waiting for transfers between devices, carried_in(): pieces = jax.tree.map(lambda part: lax.all_gather(part, axis), running)  70.9 us
    dot_general x52, matrix products, combine(): jnp.einsum('pji,pi->pj', later[0], earlier[1], precision=HIGHEST_MODE)  70.1 us
    dot_general x52, matrix products, combine(): jnp.einsum('pji,pik->pjk', later[0], earlier[0], precision=HIGHEST_MODE)  39.6 us
    add x44, other arithmetic, combine(): jnp.einsum('pji,pi->pj', later[0], earlier[1], precision=HIGHEST_MODE)  30.7 us
    dot_general x18, matrix products, apply_map(): jnp.einsum('pji,pi->pj', matrix, current, precision=HIGHEST_MODE) + vector  16.9 us
    unnamed x133, local copies, waits for them, and re-layouts  10.9 us
  transfers between devices with their start and end apart: 5, of which 2 were waited for; matrix products, arithmetic and copies ran while one was open for 23% of the time, Pallas kernels for 0%

commit v1 on v0

v1 whole, which is shorter than its diff:
```python
import functools

import jax
import jax.numpy as jnp
from jax import lax
from jax.experimental import pallas as pl
from jax.experimental.pallas import tpu as pltpu
from jax.sharding import Mesh
from jax.sharding import PartitionSpec as P

BLOCK = 128
GROUPS = 8
TM = ("x", "zh", "zl")
Z = ("zh", "zl")
INTERPRET = False
ROWS = BLOCK + 16
F32 = jnp.float32
BF16 = jnp.bfloat16


def split2(value):
    high = value.astype(BF16)
    low = (value - high.astype(F32)).astype(BF16)
    return high, low


def split3(value):
    high = value.astype(BF16)
    rest = value - high.astype(F32)
    mid = rest.astype(BF16)
    low = (rest - mid.astype(F32)).astype(BF16)
    return high, mid, low


def dot(left, right):
    return jnp.dot(left, right, preferred_element_type=F32)


def gates(rec, proj, prev, guess, ub_ref, cb_ref, par_ref):
    update = jax.nn.sigmoid(proj[0] + rec[:, 0:BLOCK] + ub_ref[...])
    reset = jax.nn.sigmoid(proj[1] + rec[:, BLOCK : 2 * BLOCK])
    inner = rec[:, 2 * BLOCK : 3 * BLOCK] + cb_ref[...]
    cand = jnp.tanh(proj[2] + reset * inner)
    mapped = (1.0 - update) * cand + update * prev
    full = (1.0 - update) * (1.0 - cand * cand) * reset
    par_ref[0] = update
    par_ref[1] = (prev - cand) * update * (1.0 - update)
    par_ref[2] = full * inner * (1.0 - reset)
    par_ref[3] = full
    par_ref[4] = mapped - guess


def advance(value, terms, rows):
    u, a, c, d = rows
    return (
        u * value
        + a * terms[:, 0:BLOCK]
        + c * terms[:, BLOCK : 2 * BLOCK]
        + d * terms[:, 2 * BLOCK : 3 * BLOCK]
    )


def advance_rows(value, double, par_ref, low, high):
    terms = dot(jnp.concatenate(split2(value), axis=1), double)
    rows = [par_ref[i, low:high, :] for i in range(4)]
    return advance(value, terms, rows) + par_ref[4, low:high, :]


def compose_all(par_ref, weight, maps_ref, send_ref, chunks, steps):
    eye = lax.broadcasted_iota(jnp.int32, (BLOCK, BLOCK), 0) == lax.broadcasted_iota(
        jnp.int32, (BLOCK, BLOCK), 1
    )
    wide = weight.astype(F32)
    double = jnp.concatenate([weight, weight], axis=0)
    part = 4
    for first in range(0, chunks, part):
        members = range(first, first + part)

        def rows_of(step, c):
            return [par_ref[i, step * chunks + c : step * chunks + c + 1, :] for i in range(4)]

        current = []
        for c in members:
            u, a, c_, d = rows_of(0, c)
            start = a * wide[:, 0:BLOCK] + c_ * wide[:, BLOCK : 2 * BLOCK] + d * wide[:, 2 * BLOCK :]
            current.append(start + jnp.where(eye, u, 0.0))
        for step in range(1, steps):
            stacked = jnp.concatenate([m.astype(BF16) for m in current], axis=0)
            terms = dot(stacked, weight)
            current = [
                advance(m, terms[k * BLOCK : (k + 1) * BLOCK], rows_of(step, c))
                for k, (m, c) in enumerate(zip(current, members))
            ]
        for m, c in zip(current, members):
            maps_ref[c, 0:BLOCK, :] = m
    vector = par_ref[4, 0:chunks, :]
    for step in range(1, steps):
        vector = advance_rows(vector, double, par_ref, step * chunks, (step + 1) * chunks)
    pad = jnp.zeros((ROWS - BLOCK - 1, BLOCK), F32)
    for c in range(chunks):
        maps_ref[c, BLOCK:ROWS, :] = jnp.concatenate([vector[c : c + 1], pad], axis=0)
    width = 1
    while width < chunks:
        for left in range(width - 1, chunks, 2 * width):
            before = jnp.concatenate(split2(maps_ref[left]), axis=1)
            for right in range(left + 1, left + 1 + width):
                high, low = split2(maps_ref[right, 0:BLOCK, :])
                upper = jnp.concatenate([high, low], axis=1)
                under = jnp.concatenate([high, jnp.zeros_like(low)], axis=1)
                both = dot(before, jnp.concatenate([upper, under], axis=0))
                both = both[:, 0:BLOCK] + both[:, BLOCK:]
                maps_ref[right, 0:BLOCK, :] = both[0:BLOCK]
                maps_ref[right, BLOCK:ROWS, :] = both[BLOCK:] + maps_ref[right, BLOCK:ROWS, :]
        width *= 2
    matrix = maps_ref[chunks - 1, 0:BLOCK, :]
    diagonal = jnp.sum(jnp.where(eye, matrix, 0.0), axis=0, keepdims=True)
    tail = [p.astype(F32) for p in split3(diagonal)]
    tail += [p.astype(F32) for p in split3(maps_ref[chunks - 1, BLOCK : BLOCK + 1, :])]
    tail.append(jnp.zeros((ROWS - BLOCK - 6, BLOCK), F32))
    matrix = jnp.where(eye, 0.0, matrix).astype(BF16)
    tail = jnp.concatenate(tail, axis=0).astype(BF16)
    for peer in range(send_ref.shape[0]):
        send_ref[peer, 0:BLOCK, :] = matrix
        send_ref[peer, BLOCK:ROWS, :] = tail


def first_maps(
    index_ref, own_ref, other_ref, w_ref, ub_ref, cb_ref,
    send_ref, maps_ref, par_ref, prev_ref, guess_ref, *, chunks, steps, blocks, stride,
):
    unit, place = index_ref[0], index_ref[1]

    def rows(ref, start):
        return ref[pl.ds(start, chunks, stride=stride), :]

    def all_steps(ref, start, jump=1):
        return jnp.concatenate([rows(ref, start + jump * s) for s in range(steps)], axis=0)

    half = blocks * BLOCK
    total = 0.0
    for ref, side in ((own_ref, unit), (other_ref, 1 - unit)):
        panels = [all_steps(ref, k * (steps + 1)).astype(BF16) for k in range(blocks)]
        columns = w_ref[pl.ds(pl.multiple_of(side * half, half), half), :]
        total = total + dot(jnp.concatenate(panels, axis=1), columns)
    base = blocks * (steps + 1)
    proj = [all_steps(own_ref, base + g, 3) for g in range(3)]
    prev = all_steps(own_ref, place * (steps + 1))
    guess = all_steps(own_ref, place * (steps + 1) + 1)
    prev_ref[...] = prev
    guess_ref[...] = guess
    gates(total, proj, prev, guess, ub_ref, cb_ref, par_ref)
    here = pl.multiple_of((unit * blocks + place) * BLOCK, BLOCK)
    compose_all(par_ref, w_ref[pl.ds(here, BLOCK), :], maps_ref, send_ref, chunks, steps)


def next_maps(
    index_ref, panel_ref, own_ref, prev_ref, guess_ref, w_ref, ub_ref, cb_ref,
    send_ref, maps_ref, par_ref, *, chunks, steps, blocks, stride,
):
    unit, place = index_ref[0], index_ref[1]
    sides = panel_ref.shape[0] // blocks
    panels = [panel_ref[k * sides + side] for side in range(sides) for k in range(blocks)]
    total = dot(jnp.concatenate(panels, axis=1), w_ref[...])
    base = blocks * (steps + 1)

    def all_steps(start):
        parts = [own_ref[pl.ds(start + 3 * s, chunks, stride=stride), :] for s in range(steps)]
        return jnp.concatenate(parts, axis=0)

    proj = [all_steps(base + g) for g in range(3)]
    gates(total, proj, prev_ref[...], guess_ref[...], ub_ref, cb_ref, par_ref)
    here = pl.multiple_of((unit * blocks + place) * BLOCK, BLOCK)
    compose_all(par_ref, w_ref[pl.ds(here, BLOCK), :], maps_ref, send_ref, chunks, steps)


def solve(index_ref, got_ref, maps_ref, par_ref, w_ref, chunks, steps, blocks):
    unit, place, group = index_ref[0], index_ref[1], index_ref[2]

    def pass_group(k, delta):
        block = got_ref[k]
        matrix = block[0:BLOCK]
        tail = block[BLOCK:ROWS].astype(F32)
        diagonal = tail[0:1] + tail[1:2] + tail[2:3]
        vector = tail[3:4] + tail[4:5] + tail[5:6]
        terms = dot(
            jnp.concatenate(split2(delta), axis=1), jnp.concatenate([matrix, matrix], axis=0)
        )
        return terms + delta * diagonal + vector

    delta = lax.fori_loop(0, group, pass_group, jnp.zeros((16, BLOCK), F32))
    column = jnp.transpose(jnp.broadcast_to(delta[0:1], (BLOCK, BLOCK)))
    entries = [delta[0:1]]
    for c in range(chunks - 1):
        through = jnp.sum(column * maps_ref[c, 0:BLOCK, :], axis=0, keepdims=True)
        entries.append(through + maps_ref[c, BLOCK : BLOCK + 1, :])
    entries = jnp.concatenate(entries, axis=0)
    here = pl.multiple_of((unit * blocks + place) * BLOCK, BLOCK)
    weight = w_ref[pl.ds(here, BLOCK), :]
    double = jnp.concatenate([weight, weight], axis=0)
    current, after = entries, []
    for step in range(steps):
        current = advance_rows(current, double, par_ref, step * chunks, (step + 1) * chunks)
        after.append(current)
    return entries, after


def first_states(
    index_ref, got_ref, maps_ref, par_ref, w_ref, prev_ref, guess_ref,
    send_ref, prev_out, guess_out, *, chunks, steps, blocks,
):
    entries, after = solve(index_ref, got_ref, maps_ref, par_ref, w_ref, chunks, steps, blocks)
    prev = prev_ref[...] + jnp.concatenate([entries] + after[:-1], axis=0)
    prev_out[...] = prev
    guess_out[...] = guess_ref[...] + jnp.concatenate(after, axis=0)
    panel = prev.astype(BF16)
    for peer in range(send_ref.shape[0]):
        send_ref[peer] = panel


def last_states(
    index_ref, got_ref, maps_ref, par_ref, w_ref, guess_ref,
    send_ref, state_ref, *, chunks, steps, blocks,
):
    quarter = index_ref[3]
    _, after = solve(index_ref, got_ref, maps_ref, par_ref, w_ref, chunks, steps, blocks)
    state_ref[...] = guess_ref[...] + jnp.concatenate(after, axis=0)
    near = send_ref.shape[0]
    for peer in range(near):
        for step in range(steps):
            row = step * chunks + quarter * near + peer
            send_ref[peer, step : step + 1, :] = state_ref[pl.ds(row, 1), :]


SMEM = pl.BlockSpec(memory_space=pltpu.SMEM)
VMEM = pl.BlockSpec(memory_space=pltpu.VMEM)


def call(body, outs, args, scratch=()):
    return pl.pallas_call(
        body,
        out_shape=[jax.ShapeDtypeStruct(shape, kind) for shape, kind in outs],
        in_specs=[SMEM] + [VMEM] * (len(args) - 1),
        out_specs=[VMEM] * len(outs),
        scratch_shapes=list(scratch),
        compiler_params=pltpu.CompilerParams(vmem_limit_bytes=24 * 1024 * 1024),
        interpret=INTERPRET,
    )(*args)


def shards(projections, recurrent, update_bias, candidate_bias, start_state, initial_guess):
    _, steps, _, width_dev = projections.shape
    full_width = recurrent.shape[0]
    blocks = width_dev // BLOCK
    chunks = lax.axis_size(Z)
    near = lax.axis_size("zl")
    sides = lax.axis_size("unit")
    groups = lax.axis_size("x")
    total_steps = chunks * steps
    place = lax.axis_index("zl")
    unit = lax.axis_index("unit")
    group = lax.axis_index("x")
    index = jnp.stack([unit, place, group, lax.axis_index("zh")]).astype(jnp.int32)

    count = lax.axis_size(TM)
    last = lax.ppermute(
        initial_guess[:, -1, :], TM, [(source, source + 1) for source in range(count - 1)]
    )
    weight = lax.dynamic_slice_in_dim(recurrent, place * BLOCK, BLOCK, 2)
    weight = jnp.concatenate([weight[:, g, :] for g in range(3)], axis=1)
    bias_u = lax.dynamic_slice_in_dim(update_bias, place * BLOCK, BLOCK, 0)[None]
    bias_c = lax.dynamic_slice_in_dim(candidate_bias, place * BLOCK, BLOCK, 0)[None]

    entering = jnp.where(lax.axis_index(TM) == 0, start_state, last)
    states = jnp.concatenate([entering, initial_guess[0]], axis=0)
    states = jnp.transpose(states.reshape(steps + 1, blocks, BLOCK), (1, 0, 2))
    states = states.reshape(blocks * (steps + 1), BLOCK)
    inputs = jnp.transpose(projections[0].reshape(steps * 3, blocks, BLOCK), (1, 0, 2))
    payload = jnp.concatenate(
        [jnp.broadcast_to(states, (blocks, *states.shape)), inputs.astype(F32)], axis=1
    )
    stride = payload.shape[1]
    payload = jnp.broadcast_to(payload, (chunks // blocks, *payload.shape))
    payload = payload.reshape(chunks, stride, BLOCK)
    own = lax.all_to_all(payload, Z, split_axis=0, concat_axis=0, tiled=True)
    other = lax.ppermute(own, "unit", [(s, sides - 1 - s) for s in range(sides)])
    own = own.reshape(chunks * stride, BLOCK)
    other = other.reshape(chunks * stride, BLOCK)

    sizes = dict(chunks=chunks, steps=steps, blocks=blocks)
    maps_out = [
        ((groups, ROWS, BLOCK), BF16),
        ((chunks, ROWS, BLOCK), F32),
        ((5, total_steps, BLOCK), F32),
    ]
    rows_out = [((total_steps, BLOCK), F32)] * 2
    send, maps, params, prev, guess = call(
        functools.partial(first_maps, stride=stride, **sizes),
        maps_out + rows_out,
        (index, own, other, weight, bias_u, bias_c),
    )
    got = lax.all_to_all(send, "x", split_axis=0, concat_axis=0, tiled=True)
    send, prev, guess = call(
        functools.partial(first_states, **sizes),
        [((near * sides, total_steps, BLOCK), BF16)] + rows_out,
        (index, got, maps, params, weight, prev, guess),
    )
    panels = lax.all_to_all(send, ("zl", "unit"), split_axis=0, concat_axis=0, tiled=True)
    send, maps, params = call(
        functools.partial(next_maps, stride=stride, **sizes),
        maps_out,
        (index, panels, own, prev, guess, weight, bias_u, bias_c),
    )
    got = lax.all_to_all(send, "x", split_axis=0, concat_axis=0, tiled=True)
    (send,) = call(
        functools.partial(last_states, **sizes),
        [((near, steps, BLOCK), F32)],
        (index, got, maps, params, weight, guess),
        [pltpu.VMEM((total_steps, BLOCK), F32)],
    )
    final = lax.all_to_all(send, "zl", split_axis=0, concat_axis=0, tiled=True)
    return jnp.transpose(final, (1, 0, 2)).reshape(1, steps, width_dev)


def solution(mesh):
    count = mesh.shape["tm"]
    near = 4
    finer = Mesh(
        mesh.devices.reshape(
            mesh.shape["sweep"], GROUPS, count // GROUPS // near, near, mesh.shape["unit"]
        ),
        ("sweep", "x", "zh", "zl", "unit"),
    )
    return jax.shard_map(
        shards,
        mesh=finer,
        in_specs=(
            P("sweep", TM, None, "unit"),
            P("sweep", None, "unit"),
            P(("sweep", "unit")),
            P(("sweep", "unit")),
            P("sweep", "unit"),
            P("sweep", TM, "unit"),
        ),
        out_specs=P("sweep", TM, "unit"),
        check_vma=False,
    )
```

time: 468 us -> 138 us (0.29); the launches traced: 458 us -> 138 us
  matrix products: 137 us -> 0 us
  blocking collectives: 156 us -> 55.3 us
  waiting for transfers between devices: 71.1 us -> 17.1 us
  other arithmetic: 49.4 us -> 1.58 us
  starting transfers between devices: 6.38 us -> 49.1 us
  local copies, waits for them, and re-layouts: 23.1 us -> 4.74 us
  between operations: 14.9 us -> 0.11 us
  Pallas kernels: 0 us -> 9.86 us
    all_gather x4 -> x0, blocking collectives: 149 us -> none  [carried_in(): pieces = jax.tree.map(lambda part: lax.all_gather(part, axis), running)]
    dot_general x132 -> x0, matrix products: 137 us -> none  [the longest x52 70.1 us: combine(): jnp.einsum('pji,pi->pj', later[0], earlier[1], precision=HIGHEST_MODE)]
    all_gather x4 -> x0, waiting for transfers between devices: 70.9 us -> none  [carried_in(): pieces = jax.tree.map(lambda part: lax.all_gather(part, axis), running)]
    all_to_all x2 -> x4, blocking collectives: 7.46 us -> 55.3 us  [the longest x2 36.1 us: shards(): got = lax.all_to_all(send, 'x', split_axis=0, concat_axis=0, tiled=True)]
    all_to_all x0 -> x1, starting transfers between devices: none -> 41.2 us  [shards(): own = lax.all_to_all(payload, Z, split_axis=0, concat_axis=0, tiled=True)]
    add x59 -> x0, other arithmetic: 38.5 us -> none  [the longest x44 30.7 us: combine(): jnp.einsum('pji,pi->pj', later[0], earlier[1], precision=HIGHEST_MODE)]
    all_to_all x0 -> x1, waiting for transfers between devices: none -> 16.4 us  [shards(): own = lax.all_to_all(payload, Z, split_axis=0, concat_axis=0, tiled=True)]
    unnamed x133 -> x1, local copies, waits for them, and re-layouts: 10.9 us -> 0.6 us
  transfers between devices with their start and end apart: 5 -> 3, of which waited for: 2 -> 3; matrix products, arithmetic and copies ran while one was open for 23% -> 2% of each run, Pallas kernels for 0% -> 0%
where the time goes in v1:
time: 138 us
  blocking collectives  55.3 us (40%)
  starting transfers between devices  49.1 us (36%)
  waiting for transfers between devices  17.1 us (12%)
  Pallas kernels  9.86 us (7%)
  local copies, waits for them, and re-layouts  4.74 us (3%)
  other arithmetic  1.58 us (1%)
    all_to_all x1, starting transfers between devices, shards(): own = lax.all_to_all(payload, Z, split_axis=0, concat_axis=0, tiled=True)  41.2 us
    all_to_all x2, blocking collectives, shards(): got = lax.all_to_all(send, 'x', split_axis=0, concat_axis=0, tiled=True)  36.1 us
    all_to_all x1, waiting for transfers between devices, shards(): own = lax.all_to_all(payload, Z, split_axis=0, concat_axis=0, tiled=True)  16.4 us
    all_to_all x1, blocking collectives, shards(): lax.all_to_all(send, ('zl', 'unit'), split_axis=0, concat_axis=0, tiled=T...  11 us
    pallas_call x4, Pallas kernels, call(): pl.pallas_call(body, out_shape=[jax.ShapeDtypeStruct(shape, kind) for sha...  9.86 us
    all_to_all x1, blocking collectives, shards(): final = lax.all_to_all(send, 'zl', split_axis=0, concat_axis=0, tiled=True)  8.23 us
    ppermute x1, starting transfers between devices, shards(): lax.ppermute(initial_guess[:, -1, :], TM, [(source, source + 1) for sourc...  6.01 us
  transfers between devices with their start and end apart: 3, of which 3 were waited for; matrix products, arithmetic and copies ran while one was open for 2% of the time, Pallas kernels for 0%

profile of v1, /device:TPU:80, one launch (start us, length us, event | category | flops | bytes accessed | tf_op | source)
XLA Modules:
  0.0 137.9 jit_solution(1552451379291715585)
XLA Ops:
  0.0 0.7 slice_bitcast_fusion
  0.7 6.0 %collective-permute-start = (f32[1,512]{1,0:T(1,128)S(1)}, f32[1,512]{1,0:T(1,128)S(1)}, u32[]{:S(2)}, u32[]{:S(2)}) collective-permute-start(f32[1,512]{1,0:T(1,128)S(1)} %slice_bitcast_fusion), channel_id=1, source_target_pairs={{0,2},{2,4},{4,6},{6,8},{8,10},{10,12},{12,14},{14,16},{16,18},{18... | collective-permute-start | bytes 6152 | tf_op jit(solution)/shard_map/ppermute | solution.py:265
  6.7 0.7 copy.9
  7.5 0.5 collective-permute-done
  8.0 0.7 fusion
  8.7 0.7 maximum_bitcast_fusion
  9.4 0.7 broadcast_in_dim.13
  10.2 41.2 %all-to-all-start = ((f32[16,32,128]{2,1,0:T(8,128)}), f32[16,32,128]{2,1,0:T(8,128)S(1)}, u32[]{:S(2)}, u32[]{:S(2)}) async-start(f32[16,32,128]{2,1,0:T(8,128)} %bitcast.10), calls=%async_computation | async-start | bytes 524288 | tf_op jit(solution)/shard_map/all_to_all | solution.py:284
  51.4 0.1 pad_add_fusion.index_ref
  51.4 0.8 dynamic-slice_bitcast_fusion.3
  52.2 16.4 %all-to-all-done = f32[16,32,128]{2,1,0:T(8,128)S(1)} async-done(((f32[16,32,128]{2,1,0:T(8,128)}), f32[16,32,128]{2,1,0:T(8,128)S(1)}, u32[]{:S(2)}, u32[]{:S(2)}) %all-to-all-start) | async-done | bytes 262176 | tf_op jit(solution)/shard_map/all_to_all | solution.py:284
  68.6 1.9 %collective-permute-start.1 = (f32[16,32,128]{2,1,0:T(8,128)S(1)}, f32[16,32,128]{2,1,0:T(8,128)S(1)}, u32[]{:S(2)}, u32[]{:S(2)}) collective-permute-start(f32[16,32,128]{2,1,0:T(8,128)S(1)} %all-to-all-done), channel_id=1, source_target_pairs={{0,1},{1,0},{2,3},{3,2},{4,5},{5,4},{6,7},{7,6},{8,9},{9,8},{10,11... | collective-permute-start | bytes 786440 | tf_op jit(solution)/shard_map/ppermute | solution.py:285
  70.6 1.2 dynamic-slice_bitcast_fusion.2
  71.8 0.1 pad_maximum_fusion.w_ref
  71.9 0.2 collective-permute-done.1
  72.1 3.8 %shard_map.64 = (bf16[8,144,128]{2,1,0:T(8,128)(2,1)S(1)}, f32[16,144,128]{2,1,0:T(8,128)S(1)}, f32[5,64,128]{2,1,0:T(8,128)S(1)}, f32[64,128]{1,0:T(8,128)S(1)}, f32[64,128]{1,0:T(8,128)S(1)}) custom-call(s32[4]{0:T(128)S(1)} %pad_add_fusion.index_ref, f32[512,128]{1,0:T(8,128)S(1)} %bitcast.30, f32[512,128]{1,0:T(8,128)S(1)} %bitcast.32, ...), custom_call_target="tpu_custom_call" | custom-call | tf_op jit(solution)/shard_map/pallas_call | solution.py:239
  75.9 21.1 %all_to_all.25.got_ref = bf16[8,144,128]{2,1,0:T(8,128)(2,1)S(1)} all-to-all(bf16[8,144,128]{2,1,0:T(8,128)(2,1)S(1)} %get-tuple-element.16), channel_id=1, replica_groups=mesh['sweep'=2,'x'=8,'zh'=4,'zl'=4,'unit'=2] {'x'}, dimensions={0} | all-to-all | bytes 589824 | tf_op jit(solution)/shard_map/all_to_all | solution.py:301
  96.9 1.2 shard_map.65
  98.1 11.0 %all_to_all.26.panel_ref = bf16[8,64,128]{2,1,0:T(8,128)(2,1)S(1)} all-to-all(bf16[8,64,128]{2,1,0:T(8,128)(2,1)S(1)} %get-tuple-element.21), channel_id=1, replica_groups=mesh['sweep'=2,'x'=8,'zh'=4,'zl'=4,'unit'=2] {'zl','unit'}, dimensions={0} | all-to-all | bytes 262144 | tf_op jit(solution)/shard_map/all_to_all | solution.py:307
  109.1 3.7 %shard_map.66 = (bf16[8,144,128]{2,1,0:T(8,128)(2,1)S(1)}, f32[16,144,128]{2,1,0:T(8,128)S(1)}, f32[5,64,128]{2,1,0:T(8,128)S(1)}) custom-call(s32[4]{0:T(128)S(1)} %pad_add_fusion.index_ref, bf16[8,64,128]{2,1,0:T(8,128)(2,1)S(1)} %all_to_all.26.panel_ref, f32[512,128]{1,0:T(8,128)S(1)} %bitcast.31, f32[64,128]{1,0:T(8,128)S(1)} %get-tuple-element.22.prev_ref, ...), custom_call_target="tpu_custom_call" | custom-call | tf_op jit(solution)/shard_map/pallas_call | solution.py:239
  112.8 15.0 %all_to_all.27.got_ref = bf16[8,144,128]{2,1,0:T(8,128)(2,1)S(1)} all-to-all(bf16[8,144,128]{2,1,0:T(8,128)(2,1)S(1)} %get-tuple-element.24), channel_id=1, replica_groups=mesh['sweep'=2,'x'=8,'zh'=4,'zl'=4,'unit'=2] {'x'}, dimensions={0} | all-to-all | bytes 589824 | tf_op jit(solution)/shard_map/all_to_all | solution.py:313
  127.8 1.2 shard_map.67
  129.0 8.2 %all_to_all.28 = f32[4,4,128]{2,1,0:T(4,128)S(1)} all-to-all(f32[4,4,128]{2,1,0:T(4,128)S(1)} %shard_map.67), channel_id=1, replica_groups=mesh['sweep'=2,'x'=8,'zh'=4,'zl'=4,'unit'=2] {'zl'}, dimensions={0} | all-to-all | bytes 16384 | tf_op jit(solution)/shard_map/all_to_all | solution.py:320
  137.3 0.6 copy.12
  (5 shorter events, 0.1 us)
Async XLA Ops:
  0.7 7.3 %collective-permute-start = (f32[1,512]{1,0:T(1,128)S(1)}, f32[1,512]{1,0:T(1,128)S(1)}, u32[]{:S(2)}, u32[]{:S(2)}) collective-permute-start(f32[1,512]{1,0:T(1,128)S(1)} %slice_bitcast_fusion), channel_id=1, source_target_pairs={{0,2},{2,4},{4,6},{6,8},{8,10},{10,12},{12,14},{14,16},{16,18},{18... | collective-permute-start | bytes 6152 | tf_op jit(solution)/shard_map/ppermute | solution.py:265
  10.2 58.5 %all-to-all-start = ((f32[16,32,128]{2,1,0:T(8,128)}), f32[16,32,128]{2,1,0:T(8,128)S(1)}, u32[]{:S(2)}, u32[]{:S(2)}) async-start(f32[16,32,128]{2,1,0:T(8,128)} %bitcast.10), calls=%async_computation | async-start | bytes 524288 | tf_op jit(solution)/shard_map/all_to_all | solution.py:284
  68.6 3.4 %collective-permute-start.1 = (f32[16,32,128]{2,1,0:T(8,128)S(1)}, f32[16,32,128]{2,1,0:T(8,128)S(1)}, u32[]{:S(2)}, u32[]{:S(2)}) collective-permute-start(f32[16,32,128]{2,1,0:T(8,128)S(1)} %all-to-all-done), channel_id=1, source_target_pairs={{0,1},{1,0},{2,3},{3,2},{4,5},{5,4},{6,7},{7,6},{8,9},{9,8},{10,11... | collective-permute-start | bytes 786440 | tf_op jit(solution)/shard_map/ppermute | solution.py:285

commit v2 on v1

--- a/solution.py
+++ b/solution.py
@@ -124,51 +124,87 @@
         send_ref[peer, BLOCK:ROWS, :] = tail
 
 
+def pack(index_ref, last_ref, start_ref, guess_ref, proj_ref, send_ref, row_ref, *, blocks):
+    steps = guess_ref.shape[0]
+    entering = jnp.where(index_ref[4] == 0, start_ref[...], last_ref[...])
+    states = jnp.concatenate([entering, guess_ref[...]], axis=0)
+    high = states.astype(BF16).astype(F32)
+    rest = states - high
+    base = (blocks + 1) * (steps + 1)
+    for target in range(blocks):
+        for k in range(blocks):
+            row_ref[target, k * (steps + 1) : (k + 1) * (steps + 1), :] = high[
+                :, k * BLOCK : (k + 1) * BLOCK
+            ]
+        lanes = slice(target * BLOCK, (target + 1) * BLOCK)
+        row_ref[target, base - steps - 1 : base, :] = rest[:, lanes]
+        for g in range(3):
+            row_ref[target, base + g * steps : base + (g + 1) * steps, :] = proj_ref[
+                g, :, lanes
+            ].astype(F32)
+        used = base + 3 * steps
+        row_ref[target, used:, :] = jnp.zeros((row_ref.shape[1] - used, BLOCK), F32)
+        packed = row_ref[target].astype(BF16)
+        for far in range(send_ref.shape[0] // blocks):
+            send_ref[far * blocks + target] = packed
+
+
 def first_maps(
     index_ref, own_ref, other_ref, w_ref, ub_ref, cb_ref,
-    send_ref, maps_ref, par_ref, prev_ref, guess_ref, *, chunks, steps, blocks, stride,
+    send_ref, maps_ref, par_ref, prev_ref, guess_ref, proj_ref, row_ref,
+    *, chunks, steps, blocks, stride,
 ):
     unit, place = index_ref[0], index_ref[1]
-
-    def rows(ref, start):
-        return ref[pl.ds(start, chunks, stride=stride), :]
-
-    def all_steps(ref, start, jump=1):
-        return jnp.concatenate([rows(ref, start + jump * s) for s in range(steps)], axis=0)
-
+    states = steps + 1
     half = blocks * BLOCK
+    base = (blocks + 1) * states
+    length = (chunks + 1) * stride
+
+    def rows(side, start):
+        return row_ref[pl.ds(side * length + start, chunks, stride=stride), :]
+
+    def before(side, start):
+        parts = [rows(side, start + steps)]
+        parts += [rows(side, stride + start + s) for s in range(1, steps)]
+        return jnp.concatenate(parts, axis=0)
+
     total = 0.0
-    for ref, side in ((own_ref, unit), (other_ref, 1 - unit)):
-        panels = [all_steps(ref, k * (steps + 1)).astype(BF16) for k in range(blocks)]
-        columns = w_ref[pl.ds(pl.multiple_of(side * half, half), half), :]
+    for side, (ref, owner) in enumerate(((own_ref, unit), (other_ref, 1 - unit))):
+        row_ref[side * length + stride : (side + 1) * length, :] = ref[...].astype(F32)
+        for k in range(blocks + 1):
+            row = side * length + k * states
+            row_ref[row + steps : row + steps + 1, :] = row_ref[row + stride : row + stride + 1, :]
+        panels = [before(side, k * states).astype(BF16) for k in range(blocks)]
+        columns = w_ref[pl.ds(pl.multiple_of(owner * half, half), half), :]
         total = total + dot(jnp.concatenate(panels, axis=1), columns)
-    base = blocks * (steps + 1)
-    proj = [all_steps(own_ref, base + g, 3) for g in range(3)]
-    prev = all_steps(own_ref, place * (steps + 1))
-    guess = all_steps(own_ref, place * (steps + 1) + 1)
+    for g in range(3):
+        start = stride + base + g * steps
+        proj_ref[g] = jnp.concatenate([rows(0, start + s) for s in range(steps)], axis=0)
+    rest = blocks * states
+    prev = before(0, place * states) + before(0, rest)
+    guess = jnp.concatenate(
+        [
+            rows(0, stride + place * states + s + 1) + rows(0, stride + rest + s + 1)
+            for s in range(steps)
+        ],
+        axis=0,
+    )
     prev_ref[...] = prev
     guess_ref[...] = guess
-    gates(total, proj, prev, guess, ub_ref, cb_ref, par_ref)
+    gates(total, proj_ref, prev, guess, ub_ref, cb_ref, par_ref)
     here = pl.multiple_of((unit * blocks + place) * BLOCK, BLOCK)
     compose_all(par_ref, w_ref[pl.ds(here, BLOCK), :], maps_ref, send_ref, chunks, steps)
 
 
 def next_maps(
-    index_ref, panel_ref, own_ref, prev_ref, guess_ref, w_ref, ub_ref, cb_ref,
-    send_ref, maps_ref, par_ref, *, chunks, steps, blocks, stride,
+    index_ref, panel_ref, proj_ref, prev_ref, guess_ref, w_ref, ub_ref, cb_ref,
+    send_ref, maps_ref, par_ref, *, chunks, steps, blocks,
 ):
     unit, place = index_ref[0], index_ref[1]
     sides = panel_ref.shape[0] // blocks
     panels = [panel_ref[k * sides + side] for side in range(sides) for k in range(blocks)]
     total = dot(jnp.concatenate(panels, axis=1), w_ref[...])
-    base = blocks * (steps + 1)
-
-    def all_steps(start):
-        parts = [own_ref[pl.ds(start + 3 * s, chunks, stride=stride), :] for s in range(steps)]
-        return jnp.concatenate(parts, axis=0)
-
-    proj = [all_steps(base + g) for g in range(3)]
-    gates(total, proj, prev_ref[...], guess_ref[...], ub_ref, cb_ref, par_ref)
+    gates(total, proj_ref, prev_ref[...], guess_ref[...], ub_ref, cb_ref, par_ref)
     here = pl.multiple_of((unit * blocks + place) * BLOCK, BLOCK)
     compose_all(par_ref, w_ref[pl.ds(here, BLOCK), :], maps_ref, send_ref, chunks, steps)
 
@@ -259,28 +295,22 @@
     place = lax.axis_index("zl")
     unit = lax.axis_index("unit")
     group = lax.axis_index("x")
-    index = jnp.stack([unit, place, group, lax.axis_index("zh")]).astype(jnp.int32)
-
-    count = lax.axis_size(TM)
-    last = lax.ppermute(
-        initial_guess[:, -1, :], TM, [(source, source + 1) for source in range(count - 1)]
-    )
+    time_place = lax.axis_index(TM)
+    index = jnp.stack([unit, place, group, lax.axis_index("zh"), time_place]).astype(jnp.int32)
+
+    links = [(chunks * k - 1, chunks * k) for k in range(1, groups)]
+    last = lax.ppermute(initial_guess[:, -1, :], TM, links)
     weight = lax.dynamic_slice_in_dim(recurrent, place * BLOCK, BLOCK, 2)
     weight = jnp.concatenate([weight[:, g, :] for g in range(3)], axis=1)
     bias_u = lax.dynamic_slice_in_dim(update_bias, place * BLOCK, BLOCK, 0)[None]
     bias_c = lax.dynamic_slice_in_dim(candidate_bias, place * BLOCK, BLOCK, 0)[None]
-
-    entering = jnp.where(lax.axis_index(TM) == 0, start_state, last)
-    states = jnp.concatenate([entering, initial_guess[0]], axis=0)
-    states = jnp.transpose(states.reshape(steps + 1, blocks, BLOCK), (1, 0, 2))
-    states = states.reshape(blocks * (steps + 1), BLOCK)
-    inputs = jnp.transpose(projections[0].reshape(steps * 3, blocks, BLOCK), (1, 0, 2))
-    payload = jnp.concatenate(
-        [jnp.broadcast_to(states, (blocks, *states.shape)), inputs.astype(F32)], axis=1
-    )
-    stride = payload.shape[1]
-    payload = jnp.broadcast_to(payload, (chunks // blocks, *payload.shape))
-    payload = payload.reshape(chunks, stride, BLOCK)
+    stride = -(-((blocks + 1) * (steps + 1) + 3 * steps) // 8) * 8
+    (payload,) = call(
+        functools.partial(pack, blocks=blocks),
+        [((chunks, stride, BLOCK), BF16)],
+        (index, last, start_state, initial_guess[0], jnp.transpose(projections[0], (1, 0, 2))),
+        [pltpu.VMEM((blocks, stride, BLOCK), F32)],
+    )
     own = lax.all_to_all(payload, Z, split_axis=0, concat_axis=0, tiled=True)
     other = lax.ppermute(own, "unit", [(s, sides - 1 - s) for s in range(sides)])
     own = own.reshape(chunks * stride, BLOCK)
@@ -293,10 +323,11 @@
         ((5, total_steps, BLOCK), F32),
     ]
     rows_out = [((total_steps, BLOCK), F32)] * 2
-    send, maps, params, prev, guess = call(
+    send, maps, params, prev, guess, proj = call(
         functools.partial(first_maps, stride=stride, **sizes),
-        maps_out + rows_out,
+        maps_out + rows_out + [((3, total_steps, BLOCK), F32)],
         (index, own, other, weight, bias_u, bias_c),
+        [pltpu.VMEM((sides * (chunks + 1) * stride, BLOCK), F32)],
     )
     got = lax.all_to_all(send, "x", split_axis=0, concat_axis=0, tiled=True)
     send, prev, guess = call(
@@ -306,9 +337,9 @@
     )
     panels = lax.all_to_all(send, ("zl", "unit"), split_axis=0, concat_axis=0, tiled=True)
     send, maps, params = call(
-        functools.partial(next_maps, stride=stride, **sizes),
+        functools.partial(next_maps, **sizes),
         maps_out,
-        (index, panels, own, prev, guess, weight, bias_u, bias_c),
+        (index, panels, proj, prev, guess, weight, bias_u, bias_c),
     )
     got = lax.all_to_all(send, "x", split_axis=0, concat_axis=0, tiled=True)
     (send,) = call(

time: 138 us -> 136 us (0.986)
  waiting for transfers between devices: 17.1 us -> 14.1 us
  other arithmetic: 1.58 us -> 0.1 us
    ppermute x1, starting transfers between devices: 6.01 us -> 0.65 us  [shards(): last = lax.ppermute(initial_guess[:, -1, :], TM, links)]
    all_to_all x1, starting transfers between devices: 41.2 us -> 45.5 us  [shards(): own = lax.all_to_all(payload, Z, split_axis=0, concat_axis=0, tiled=True)]
    all_to_all x1, waiting for transfers between devices: 16.4 us -> 13.6 us  [shards(): own = lax.all_to_all(payload, Z, split_axis=0, concat_axis=0, tiled=True)]
    unnamed x1 -> x7, local copies, waits for them, and re-layouts: 0.6 us -> 2.68 us
    pallas_call x4 -> x5, Pallas kernels: 9.86 us -> 11 us  [call(): pl.pallas_call(body, out_shape=[jax.ShapeDtypeStruct(shape, kind) for sha...]
  transfers between devices with their start and end apart: 3 -> 3, of which waited for: 3 -> 2; matrix products, arithmetic and copies ran while one was open for 2% -> 2% of each run, Pallas kernels for 0% -> 0%
where the time goes in v2:
time: 136 us; the launch traced here: 135 us
  blocking collectives  56.1 us (41%)
  starting transfers between devices  48.1 us (35%)
  waiting for transfers between devices  14.1 us (10%)
  Pallas kernels  11 us (8%)
  local copies, waits for them, and re-layouts  5.43 us (4%)
    all_to_all x1, starting transfers between devices, shards(): own = lax.all_to_all(payload, Z, split_axis=0, concat_axis=0, tiled=True)  45.5 us
    all_to_all x2, blocking collectives, shards(): got = lax.all_to_all(send, 'x', split_axis=0, concat_axis=0, tiled=True)  37.2 us
    all_to_all x1, waiting for transfers between devices, shards(): own = lax.all_to_all(payload, Z, split_axis=0, concat_axis=0, tiled=True)  13.6 us
    pallas_call x5, Pallas kernels, call(): pl.pallas_call(body, out_shape=[jax.ShapeDtypeStruct(shape, kind) for sha...  11 us
    all_to_all x1, blocking collectives, shards(): lax.all_to_all(send, ('zl', 'unit'), split_axis=0, concat_axis=0, tiled=T...  10.6 us
    all_to_all x1, blocking collectives, shards(): final = lax.all_to_all(send, 'zl', split_axis=0, concat_axis=0, tiled=True)  8.23 us
  transfers between devices with their start and end apart: 3, of which 2 were waited for; matrix products, arithmetic and copies ran while one was open for 2% of the time, Pallas kernels for 0%

profile of v2, /device:TPU:80, one launch (start us, length us, event | category | flops | bytes accessed | tf_op | source)
XLA Modules:
  0.0 134.9 jit_solution(12465647115568199434)
XLA Ops:
  0.0 0.7 slice_bitcast_fusion
  0.7 0.6 collective-permute-start
  1.4 0.1 stack.23.index_ref
  1.5 0.0 collective-permute-done.last_ref
  1.5 0.0 copy-start
  1.5 0.7 copy-done
  2.2 0.0 copy-start.1
  2.2 0.7 copy-done.1
  2.9 0.0 copy-start.2
  2.9 0.7 copy-done.2
  3.5 1.2 shard_map.64
  4.8 45.5 %all-to-all-start = ((bf16[16,40,128]{2,1,0:T(8,128)(2,1)}), bf16[16,40,128]{2,1,0:T(8,128)(2,1)S(1)}, u32[]{:S(2)}, u32[]{:S(2)}) async-start(bf16[16,40,128]{2,1,0:T(8,128)(2,1)} %shard_map.64), calls=%async_computation | async-start | bytes 327680 | tf_op jit(solution)/shard_map/all_to_all | solution.py:314
  50.3 1.2 dynamic-slice_bitcast_fusion.2
  51.5 13.6 %all-to-all-done = bf16[16,40,128]{2,1,0:T(8,128)(2,1)S(1)} async-done(((bf16[16,40,128]{2,1,0:T(8,128)(2,1)}), bf16[16,40,128]{2,1,0:T(8,128)(2,1)S(1)}, u32[]{:S(2)}, u32[]{:S(2)}) %all-to-all-start) | async-done | bytes 163872 | tf_op jit(solution)/shard_map/all_to_all | solution.py:314
  65.1 1.9 %collective-permute-start.1 = (bf16[16,40,128]{2,1,0:T(8,128)(2,1)S(1)}, bf16[16,40,128]{2,1,0:T(8,128)(2,1)S(1)}, u32[]{:S(2)}, u32[]{:S(2)}) collective-permute-start(bf16[16,40,128]{2,1,0:T(8,128)(2,1)S(1)} %all-to-all-done), channel_id=1, source_target_pairs={{0,1},{1,0},{2,3},{3,2},{4,5},{5,4},{6,7},{7,6},{8,9},{9,8},{10,11... | collective-permute-start | bytes 491528 | tf_op jit(solution)/shard_map/ppermute | solution.py:315
  67.1 0.8 dynamic-slice_bitcast_fusion.3
  67.8 0.1 pad_maximum_fusion.w_ref
  68.0 0.5 collective-permute-done.1
  68.4 3.7 %shard_map.65 = (bf16[8,144,128]{2,1,0:T(8,128)(2,1)S(1)}, f32[16,144,128]{2,1,0:T(8,128)S(1)}, f32[5,64,128]{2,1,0:T(8,128)S(1)}, f32[64,128]{1,0:T(8,128)S(1)}...) custom-call(s32[5]{0:T(128)S(1)} %stack.23.index_ref, bf16[640,128]{1,0:T(8,128)(2,1)S(1)} %bitcast.26, ...), custom_call_target="tpu_custom_call" | custom-call | tf_op jit(solution)/shard_map/pallas_call | solution.py:275
  72.1 22.3 %all_to_all.25.got_ref = bf16[8,144,128]{2,1,0:T(8,128)(2,1)S(1)} all-to-all(bf16[8,144,128]{2,1,0:T(8,128)(2,1)S(1)} %get-tuple-element.17), channel_id=1, replica_groups=mesh['sweep'=2,'x'=8,'zh'=4,'zl'=4,'unit'=2] {'x'}, dimensions={0} | all-to-all | bytes 589824 | tf_op jit(solution)/shard_map/all_to_all | solution.py:332
  94.4 1.2 shard_map.66
  95.6 10.6 %all_to_all.26.panel_ref = bf16[8,64,128]{2,1,0:T(8,128)(2,1)S(1)} all-to-all(bf16[8,64,128]{2,1,0:T(8,128)(2,1)S(1)} %get-tuple-element.22), channel_id=1, replica_groups=mesh['sweep'=2,'x'=8,'zh'=4,'zl'=4,'unit'=2] {'zl','unit'}, dimensions={0} | all-to-all | bytes 262144 | tf_op jit(solution)/shard_map/all_to_all | solution.py:338
  106.2 3.7 %shard_map.67 = (bf16[8,144,128]{2,1,0:T(8,128)(2,1)S(1)}, f32[16,144,128]{2,1,0:T(8,128)S(1)}, f32[5,64,128]{2,1,0:T(8,128)S(1)}) custom-call(s32[5]{0:T(128)S(1)} %stack.23.index_ref, bf16[8,64,128]{2,1,0:T(8,128)(2,1)S(1)} %all_to_all.26.panel_ref, f32[3,64,128]{2,1,0:T(8,128)S(1)} %get-tuple-element.23.proj_ref, ...), custom_call_target="tpu_custom_call" | custom-call | tf_op jit(solution)/shard_map/pallas_call | solution.py:275
  109.9 15.0 %all_to_all.27.got_ref = bf16[8,144,128]{2,1,0:T(8,128)(2,1)S(1)} all-to-all(bf16[8,144,128]{2,1,0:T(8,128)(2,1)S(1)} %get-tuple-element.26), channel_id=1, replica_groups=mesh['sweep'=2,'x'=8,'zh'=4,'zl'=4,'unit'=2] {'x'}, dimensions={0} | all-to-all | bytes 589824 | tf_op jit(solution)/shard_map/all_to_all | solution.py:344
  124.8 1.2 shard_map.68
  126.1 8.2 %all_to_all.28 = f32[4,4,128]{2,1,0:T(4,128)S(1)} all-to-all(f32[4,4,128]{2,1,0:T(4,128)S(1)} %shard_map.68), channel_id=1, replica_groups=mesh['sweep'=2,'x'=8,'zh'=4,'zl'=4,'unit'=2] {'zl'}, dimensions={0} | all-to-all | bytes 16384 | tf_op jit(solution)/shard_map/all_to_all | solution.py:351
  134.3 0.6 copy.8
Async XLA Ops:
  0.7 0.8 collective-permute-start
  1.5 0.7 copy-start
  2.2 0.7 copy-start.1
  2.9 0.7 copy-start.2
  4.8 60.3 %all-to-all-start = ((bf16[16,40,128]{2,1,0:T(8,128)(2,1)}), bf16[16,40,128]{2,1,0:T(8,128)(2,1)S(1)}, u32[]{:S(2)}, u32[]{:S(2)}) async-start(bf16[16,40,128]{2,1,0:T(8,128)(2,1)} %shard_map.64), calls=%async_computation | async-start | bytes 327680 | tf_op jit(solution)/shard_map/all_to_all | solution.py:314
  65.1 3.3 %collective-permute-start.1 = (bf16[16,40,128]{2,1,0:T(8,128)(2,1)S(1)}, bf16[16,40,128]{2,1,0:T(8,128)(2,1)S(1)}, u32[]{:S(2)}, u32[]{:S(2)}) collective-permute-start(bf16[16,40,128]{2,1,0:T(8,128)(2,1)S(1)} %all-to-all-done), channel_id=1, source_target_pairs={{0,1},{1,0},{2,3},{3,2},{4,5},{5,4},{6,7},{7,6},{8,9},{9,8},{10,11... | collective-permute-start | bytes 491528 | tf_op jit(solution)/shard_map/ppermute | solution.py:315

commit v3 on v2

--- a/solution.py
+++ b/solution.py
@@ -66,7 +66,7 @@
     return advance(value, terms, rows) + par_ref[4, low:high, :]
 
 
-def compose_all(par_ref, weight, maps_ref, send_ref, chunks, steps):
+def compose_all(par_ref, weight, maps_ref, send_ref, chunks, steps, entry=None):
     eye = lax.broadcasted_iota(jnp.int32, (BLOCK, BLOCK), 0) == lax.broadcasted_iota(
         jnp.int32, (BLOCK, BLOCK), 1
     )
@@ -94,6 +94,9 @@
         for m, c in zip(current, members):
             maps_ref[c, 0:BLOCK, :] = m
     vector = par_ref[4, 0:chunks, :]
+    if entry is not None:
+        vector = jnp.concatenate([entry, jnp.zeros((chunks - 1, BLOCK), F32)], axis=0)
+        vector = advance_rows(vector, double, par_ref, 0, chunks)
     for step in range(1, steps):
         vector = advance_rows(vector, double, par_ref, step * chunks, (step + 1) * chunks)
     pad = jnp.zeros((ROWS - BLOCK - 1, BLOCK), F32)
@@ -124,25 +127,38 @@
         send_ref[peer, BLOCK:ROWS, :] = tail
 
 
-def pack(index_ref, last_ref, start_ref, guess_ref, proj_ref, send_ref, row_ref, *, blocks):
+def pack(
+    guess_hbm, proj_hbm, start_hbm, send_ref, row_ref, guess_ref, proj_ref, start_ref, sems, *, blocks
+):
+    copies = [
+        pltpu.make_async_copy(source, target, sems.at[i])
+        for i, (source, target) in enumerate(
+            ((guess_hbm, guess_ref), (proj_hbm, proj_ref), (start_hbm, start_ref))
+        )
+    ]
+    for copy in copies:
+        copy.start()
+    for copy in copies:
+        copy.wait()
     steps = guess_ref.shape[0]
-    entering = jnp.where(index_ref[4] == 0, start_ref[...], last_ref[...])
-    states = jnp.concatenate([entering, guess_ref[...]], axis=0)
-    high = states.astype(BF16).astype(F32)
-    rest = states - high
-    base = (blocks + 1) * (steps + 1)
+    high = guess_ref[...].astype(BF16).astype(F32)
+    rest = guess_ref[...] - high
+    start_high = start_ref[...].astype(BF16).astype(F32)
+    start_rest = start_ref[...] - start_high
+    inputs = (blocks + 1) * steps
+    first = inputs + 3 * steps
+    used = first + blocks + 1
     for target in range(blocks):
+        lanes = slice(target * BLOCK, (target + 1) * BLOCK)
         for k in range(blocks):
-            row_ref[target, k * (steps + 1) : (k + 1) * (steps + 1), :] = high[
-                :, k * BLOCK : (k + 1) * BLOCK
-            ]
-        lanes = slice(target * BLOCK, (target + 1) * BLOCK)
-        row_ref[target, base - steps - 1 : base, :] = rest[:, lanes]
+            there = slice(k * BLOCK, (k + 1) * BLOCK)
+            row_ref[target, k * steps : (k + 1) * steps, :] = high[:, there]
+            row_ref[target, first + k : first + k + 1, :] = start_high[:, there]
+        row_ref[target, blocks * steps : inputs, :] = rest[:, lanes]
         for g in range(3):
-            row_ref[target, base + g * steps : base + (g + 1) * steps, :] = proj_ref[
-                g, :, lanes
-            ].astype(F32)
-        used = base + 3 * steps
+            begin = inputs + g * steps
+            row_ref[target, begin : begin + steps, :] = proj_ref[g, :, lanes].astype(F32)
+        row_ref[target, used - 1 : used, :] = start_rest[:, lanes]
         row_ref[target, used:, :] = jnp.zeros((row_ref.shape[1] - used, BLOCK), F32)
         packed = row_ref[target].astype(BF16)
         for far in range(send_ref.shape[0] // blocks):
@@ -150,50 +166,59 @@
 
 
 def first_maps(
-    index_ref, own_ref, other_ref, w_ref, ub_ref, cb_ref,
+    index_ref, own_ref, other_ref, next_ref, w_ref, ub_ref, cb_ref,
     send_ref, maps_ref, par_ref, prev_ref, guess_ref, proj_ref, row_ref,
     *, chunks, steps, blocks, stride,
 ):
-    unit, place = index_ref[0], index_ref[1]
-    states = steps + 1
+    unit, place, group = index_ref[0], index_ref[1], index_ref[2]
     half = blocks * BLOCK
-    base = (blocks + 1) * states
+    inputs = (blocks + 1) * steps
+    first = inputs + 3 * steps
     length = (chunks + 1) * stride
+    total_steps = chunks * steps
+    extra = 16
 
     def rows(side, start):
         return row_ref[pl.ds(side * length + start, chunks, stride=stride), :]
 
-    def before(side, start):
-        parts = [rows(side, start + steps)]
-        parts += [rows(side, stride + start + s) for s in range(1, steps)]
-        return jnp.concatenate(parts, axis=0)
-
+    def all_steps(side, start):
+        return [rows(side, start + s) for s in range(steps)]
+
+    def later(start):
+        return [rows(0, start + s) for s in range(1, steps)] + [rows(0, stride + start)]
+
+    def one(start, side=0):
+        row = row_ref[pl.ds(side * length + start, 1), :]
+        return jnp.broadcast_to(row, (extra, BLOCK))
+
+    row_ref[length - stride : length, :] = next_ref[...].astype(F32)
     total = 0.0
     for side, (ref, owner) in enumerate(((own_ref, unit), (other_ref, 1 - unit))):
-        row_ref[side * length + stride : (side + 1) * length, :] = ref[...].astype(F32)
-        for k in range(blocks + 1):
-            row = side * length + k * states
-            row_ref[row + steps : row + steps + 1, :] = row_ref[row + stride : row + stride + 1, :]
-        panels = [before(side, k * states).astype(BF16) for k in range(blocks)]
+        row_ref[side * length : side * length + chunks * stride, :] = ref[...].astype(F32)
+        panels = [
+            jnp.concatenate(all_steps(side, k * steps) + [one(first + k, side)], axis=0).astype(BF16)
+            for k in range(blocks)
+        ]
         columns = w_ref[pl.ds(pl.multiple_of(owner * half, half), half), :]
         total = total + dot(jnp.concatenate(panels, axis=1), columns)
+    proj = []
     for g in range(3):
-        start = stride + base + g * steps
-        proj_ref[g] = jnp.concatenate([rows(0, start + s) for s in range(steps)], axis=0)
-    rest = blocks * states
-    prev = before(0, place * states) + before(0, rest)
-    guess = jnp.concatenate(
-        [
-            rows(0, stride + place * states + s + 1) + rows(0, stride + rest + s + 1)
-            for s in range(steps)
-        ],
-        axis=0,
-    )
-    prev_ref[...] = prev
-    guess_ref[...] = guess
-    gates(total, proj_ref, prev, guess, ub_ref, cb_ref, par_ref)
+        start = inputs + g * steps
+        proj.append(jnp.concatenate(later(start) + [one(start)], axis=0))
+        proj_ref[g] = proj[g][0:total_steps]
+    own, rest = place * steps, blocks * steps
+    begin = one(first + place) + one(first + blocks)
+    prev = jnp.concatenate(all_steps(0, own) + [begin], axis=0)
+    prev += jnp.concatenate(all_steps(0, rest) + [jnp.zeros_like(begin)], axis=0)
+    guess = jnp.concatenate(later(own) + [one(own)], axis=0)
+    guess += jnp.concatenate(later(rest) + [one(rest)], axis=0)
+    prev_ref[...] = prev[0:total_steps]
+    guess_ref[...] = guess[0:total_steps]
+    gates(total, proj, prev, guess, ub_ref, cb_ref, par_ref)
+    entry = jnp.where(group == 0, par_ref[4, total_steps : total_steps + 1, :], 0.0)
+    par_ref[4, total_steps : total_steps + 1, :] = entry
     here = pl.multiple_of((unit * blocks + place) * BLOCK, BLOCK)
-    compose_all(par_ref, w_ref[pl.ds(here, BLOCK), :], maps_ref, send_ref, chunks, steps)
+    compose_all(par_ref, w_ref[pl.ds(here, BLOCK), :], maps_ref, send_ref, chunks, steps, entry)
 
 
 def next_maps(
@@ -209,7 +234,7 @@
     compose_all(par_ref, w_ref[pl.ds(here, BLOCK), :], maps_ref, send_ref, chunks, steps)
 
 
-def solve(index_ref, got_ref, maps_ref, par_ref, w_ref, chunks, steps, blocks):
+def solve(index_ref, got_ref, maps_ref, par_ref, w_ref, chunks, steps, blocks, entry=0.0):
     unit, place, group = index_ref[0], index_ref[1], index_ref[2]
 
     def pass_group(k, delta):
@@ -225,7 +250,7 @@
 
     delta = lax.fori_loop(0, group, pass_group, jnp.zeros((16, BLOCK), F32))
     column = jnp.transpose(jnp.broadcast_to(delta[0:1], (BLOCK, BLOCK)))
-    entries = [delta[0:1]]
+    entries = [delta[0:1] + entry]
     for c in range(chunks - 1):
         through = jnp.sum(column * maps_ref[c, 0:BLOCK, :], axis=0, keepdims=True)
         entries.append(through + maps_ref[c, BLOCK : BLOCK + 1, :])
@@ -244,7 +269,10 @@
     index_ref, got_ref, maps_ref, par_ref, w_ref, prev_ref, guess_ref,
     send_ref, prev_out, guess_out, *, chunks, steps, blocks,
 ):
-    entries, after = solve(index_ref, got_ref, maps_ref, par_ref, w_ref, chunks, steps, blocks)
+    entry = par_ref[4, chunks * steps : chunks * steps + 1, :]
+    entries, after = solve(
+        index_ref, got_ref, maps_ref, par_ref, w_ref, chunks, steps, blocks, entry
+    )
     prev = prev_ref[...] + jnp.concatenate([entries] + after[:-1], axis=0)
     prev_out[...] = prev
     guess_out[...] = guess_ref[...] + jnp.concatenate(after, axis=0)
@@ -254,12 +282,12 @@
 
 
 def last_states(
-    index_ref, got_ref, maps_ref, par_ref, w_ref, guess_ref,
+    index_ref, got_ref, maps_ref, par_ref, w_ref, prev_ref,
     send_ref, state_ref, *, chunks, steps, blocks,
 ):
     quarter = index_ref[3]
-    _, after = solve(index_ref, got_ref, maps_ref, par_ref, w_ref, chunks, steps, blocks)
-    state_ref[...] = guess_ref[...] + jnp.concatenate(after, axis=0)
+    entries, after = solve(index_ref, got_ref, maps_ref, par_ref, w_ref, chunks, steps - 1, blocks)
+    state_ref[...] = prev_ref[...] + jnp.concatenate([entries] + after, axis=0)
     near = send_ref.shape[0]
     for peer in range(near):
         for step in range(steps):
@@ -271,14 +299,14 @@
 VMEM = pl.BlockSpec(memory_space=pltpu.VMEM)
 
 
-def call(body, outs, args, scratch=()):
+def call(body, outs, args, scratch=(), first=SMEM, rest=VMEM, limit=24 * 1024 * 1024):
     return pl.pallas_call(
         body,
         out_shape=[jax.ShapeDtypeStruct(shape, kind) for shape, kind in outs],
-        in_specs=[SMEM] + [VMEM] * (len(args) - 1),
+        in_specs=[first] + [rest] * (len(args) - 1),
         out_specs=[VMEM] * len(outs),
         scratch_shapes=list(scratch),
-        compiler_params=pltpu.CompilerParams(vmem_limit_bytes=24 * 1024 * 1024),
+        compiler_params=pltpu.CompilerParams(vmem_limit_bytes=limit),
         interpret=INTERPRET,
     )(*args)
 
@@ -295,23 +323,31 @@
     place = lax.axis_index("zl")
     unit = lax.axis_index("unit")
     group = lax.axis_index("x")
-    time_place = lax.axis_index(TM)
-    index = jnp.stack([unit, place, group, lax.axis_index("zh"), time_place]).astype(jnp.int32)
-
-    links = [(chunks * k - 1, chunks * k) for k in range(1, groups)]
-    last = lax.ppermute(initial_guess[:, -1, :], TM, links)
+    index = jnp.stack([unit, place, group, lax.axis_index("zh")]).astype(jnp.int32)
+
     weight = lax.dynamic_slice_in_dim(recurrent, place * BLOCK, BLOCK, 2)
     weight = jnp.concatenate([weight[:, g, :] for g in range(3)], axis=1)
     bias_u = lax.dynamic_slice_in_dim(update_bias, place * BLOCK, BLOCK, 0)[None]
     bias_c = lax.dynamic_slice_in_dim(candidate_bias, place * BLOCK, BLOCK, 0)[None]
     stride = -(-((blocks + 1) * (steps + 1) + 3 * steps) // 8) * 8
+    here = pl.BlockSpec(memory_space=pl.ANY)
     (payload,) = call(
         functools.partial(pack, blocks=blocks),
         [((chunks, stride, BLOCK), BF16)],
-        (index, last, start_state, initial_guess[0], jnp.transpose(projections[0], (1, 0, 2))),
-        [pltpu.VMEM((blocks, stride, BLOCK), F32)],
+        (initial_guess[0], jnp.transpose(projections[0], (1, 0, 2)), start_state),
+        [
+            pltpu.VMEM((blocks, stride, BLOCK), F32),
+            pltpu.VMEM((steps, width_dev), F32),
+            pltpu.VMEM((3, steps, width_dev), BF16),
+            pltpu.VMEM((1, width_dev), F32),
+            pltpu.SemaphoreType.DMA((3,)),
+        ],
+        here,
+        here,
+        60 * 1024 * 1024,
     )
     own = lax.all_to_all(payload, Z, split_axis=0, concat_axis=0, tiled=True)
+    after = lax.ppermute(own[0], "x", [(k + 1, k) for k in range(groups - 1)])
     other = lax.ppermute(own, "unit", [(s, sides - 1 - s) for s in range(sides)])
     own = own.reshape(chunks * stride, BLOCK)
     other = other.reshape(chunks * stride, BLOCK)
@@ -323,10 +359,11 @@
         ((5, total_steps, BLOCK), F32),
     ]
     rows_out = [((total_steps, BLOCK), F32)] * 2
+    first_out = maps_out[:2] + [((5, total_steps + 16, BLOCK), F32)]
     send, maps, params, prev, guess, proj = call(
         functools.partial(first_maps, stride=stride, **sizes),
-        maps_out + rows_out + [((3, total_steps, BLOCK), F32)],
-        (index, own, other, weight, bias_u, bias_c),
+        first_out + rows_out + [((3, total_steps, BLOCK), F32)],
+        (index, own, other, after, weight, bias_u, bias_c),
         [pltpu.VMEM((sides * (chunks + 1) * stride, BLOCK), F32)],
     )
     got = lax.all_to_all(send, "x", split_axis=0, concat_axis=0, tiled=True)
@@ -345,7 +382,7 @@
     (send,) = call(
         functools.partial(last_states, **sizes),
         [((near, steps, BLOCK), F32)],
-        (index, got, maps, params, weight, guess),
+        (index, got, maps, params, weight, prev),
         [pltpu.VMEM((total_steps, BLOCK), F32)],
     )
     final = lax.all_to_all(send, "zl", split_axis=0, concat_axis=0, tiled=True)

time: 136 us -> 131 us (0.963)
  blocking collectives: 56.1 us -> 52.6 us
  waiting for transfers between devices: 14.1 us -> 17.4 us
  local copies, waits for them, and re-layouts: 5.43 us -> 2.56 us
    ppermute x1, waiting for transfers between devices: 0.01 us -> 4.2 us  [shards(): after = lax.ppermute(own[0], 'x', [(k + 1, k) for k in range(groups - 1)])]
    all_to_all x2, blocking collectives: 37.2 us -> 34.2 us  [shards(): got = lax.all_to_all(send, 'x', split_axis=0, concat_axis=0, tiled=True)]
    unnamed x7 -> x1, local copies, waits for them, and re-layouts: 2.68 us -> 0.6 us
    all_to_all x1, starting transfers between devices: 45.5 us -> 43.7 us  [shards(): own = lax.all_to_all(payload, Z, split_axis=0, concat_axis=0, tiled=True)]
where the time goes in v3:
time: 131 us
  blocking collectives  52.6 us (40%)
  starting transfers between devices  46.9 us (36%)
  waiting for transfers between devices  17.4 us (13%)
  Pallas kernels  11.2 us (9%)
  local copies, waits for them, and re-layouts  2.56 us (2%)
    all_to_all x1, starting transfers between devices, shards(): own = lax.all_to_all(payload, Z, split_axis=0, concat_axis=0, tiled=True)  43.7 us
    all_to_all x2, blocking collectives, shards(): got = lax.all_to_all(send, 'x', split_axis=0, concat_axis=0, tiled=True)  34.2 us
    all_to_all x1, waiting for transfers between devices, shards(): own = lax.all_to_all(payload, Z, split_axis=0, concat_axis=0, tiled=True)  13.2 us
    pallas_call x5, Pallas kernels, call(): pl.pallas_call(body, out_shape=[jax.ShapeDtypeStruct(shape, kind) for sha...  11.2 us
    all_to_all x1, blocking collectives, shards(): lax.all_to_all(send, ('zl', 'unit'), split_axis=0, concat_axis=0, tiled=T...  10.2 us
    all_to_all x1, blocking collectives, shards(): final = lax.all_to_all(send, 'zl', split_axis=0, concat_axis=0, tiled=True)  8.23 us
    ppermute x1, waiting for transfers between devices, shards(): after = lax.ppermute(own[0], 'x', [(k + 1, k) for k in range(groups - 1)])  4.2 us
  transfers between devices with their start and end apart: 3, of which 2 were waited for; matrix products, arithmetic and copies ran while one was open for 2% of the time, Pallas kernels for 0%

profile of v3, /device:TPU:80, one launch (start us, length us, event | category | flops | bytes accessed | tf_op | source)
XLA Modules:
  0.0 130.9 jit_solution(5420069988939550728)
XLA Ops:
  0.0 1.4 %shard_map.64 = bf16[16,40,128]{2,1,0:T(8,128)(2,1)} custom-call(f32[4,512]{1,0:T(4,128)} %bitcast.29, bf16[3,4,512]{2,1,0:T(4,128)(2,1)} %bitcast.28, f32[1,512]{1,0:T(1,128)} %start_hbm.1), custom_call_target="tpu_custom_call" | custom-call | tf_op jit(solution)/shard_map/pallas_call | solution.py:303
  1.4 43.7 %all-to-all-start = ((bf16[16,40,128]{2,1,0:T(8,128)(2,1)}), bf16[16,40,128]{2,1,0:T(8,128)(2,1)S(1)}, u32[]{:S(2)}, u32[]{:S(2)}) async-start(bf16[16,40,128]{2,1,0:T(8,128)(2,1)} %shard_map.64), calls=%async_computation | async-start | bytes 327680 | tf_op jit(solution)/shard_map/all_to_all | solution.py:349
  45.1 0.8 dynamic-slice_bitcast_fusion.3
  45.9 1.2 dynamic-slice_bitcast_fusion.2
  47.1 0.1 pad_maximum_fusion.w_ref
  47.2 13.2 %all-to-all-done = bf16[16,40,128]{2,1,0:T(8,128)(2,1)S(1)} async-done(((bf16[16,40,128]{2,1,0:T(8,128)(2,1)}), bf16[16,40,128]{2,1,0:T(8,128)(2,1)S(1)}, u32[]{:S(2)}, u32[]{:S(2)}) %all-to-all-start) | async-done | bytes 163872 | tf_op jit(solution)/shard_map/all_to_all | solution.py:349
  60.5 1.9 %collective-permute-start = (bf16[16,40,128]{2,1,0:T(8,128)(2,1)S(1)}, bf16[16,40,128]{2,1,0:T(8,128)(2,1)S(1)}, u32[]{:S(2)}, u32[]{:S(2)}) collective-permute-start(bf16[16,40,128]{2,1,0:T(8,128)(2,1)S(1)} %all-to-all-done), channel_id=1, source_target_pairs={{0,1},{1,0},{2,3},{3,2},{4,5},{5,4},{6,7},{7,6},{8,9},{9,8},{10,11... | collective-permute-start | bytes 491528 | tf_op jit(solution)/shard_map/ppermute | solution.py:351
  62.4 1.3 collective-permute-start.1
  63.7 0.1 pad_add_fusion.index_ref
  63.8 4.2 %collective-permute-done.1.next_ref = bf16[40,128]{1,0:T(8,128)(2,1)S(1)} collective-permute-done((bf16[40,128]{1,0:T(8,128)(2,1)S(1)}, bf16[40,128]{1,0:T(8,128)(2,1)S(1)}, u32[]{:S(2)}, u32[]{:S(2)}) %collective-permute-start.1) | collective-permute-done | bytes 10272 | tf_op jit(solution)/shard_map/ppermute | solution.py:350
  68.0 0.0 collective-permute-done
  68.0 3.8 %shard_map.65 = (bf16[8,144,128]{2,1,0:T(8,128)(2,1)S(1)}, f32[16,144,128]{2,1,0:T(8,128)S(1)}, f32[5,80,128]{2,1,0:T(8,128)S(1)}, f32[64,128]{1,0:T(8,128)S(1)}...) custom-call(s32[4]{0:T(128)S(1)} %pad_add_fusion.index_ref, bf16[640,128]{1,0:T(8,128)(2,1)S(1)} %bitcast.25, ...), custom_call_target="tpu_custom_call" | custom-call | tf_op jit(solution)/shard_map/pallas_call | solution.py:303
  71.8 19.2 %all_to_all.25.got_ref = bf16[8,144,128]{2,1,0:T(8,128)(2,1)S(1)} all-to-all(bf16[8,144,128]{2,1,0:T(8,128)(2,1)S(1)} %get-tuple-element.17), channel_id=1, replica_groups=mesh['sweep'=2,'x'=8,'zh'=4,'zl'=4,'unit'=2] {'x'}, dimensions={0} | all-to-all | bytes 589824 | tf_op jit(solution)/shard_map/all_to_all | solution.py:369
  91.0 1.2 shard_map.66
  92.2 10.2 %all_to_all.26.panel_ref = bf16[8,64,128]{2,1,0:T(8,128)(2,1)S(1)} all-to-all(bf16[8,64,128]{2,1,0:T(8,128)(2,1)S(1)} %get-tuple-element.22), channel_id=1, replica_groups=mesh['sweep'=2,'x'=8,'zh'=4,'zl'=4,'unit'=2] {'zl','unit'}, dimensions={0} | all-to-all | bytes 262144 | tf_op jit(solution)/shard_map/all_to_all | solution.py:375
  102.4 3.7 %shard_map.67 = (bf16[8,144,128]{2,1,0:T(8,128)(2,1)S(1)}, f32[16,144,128]{2,1,0:T(8,128)S(1)}, f32[5,64,128]{2,1,0:T(8,128)S(1)}) custom-call(s32[4]{0:T(128)S(1)} %pad_add_fusion.index_ref, bf16[8,64,128]{2,1,0:T(8,128)(2,1)S(1)} %all_to_all.26.panel_ref, f32[3,64,128]{2,1,0:T(8,128)S(1)} %get-tuple-element.23.proj_ref, ...), custom_call_target="tpu_custom_call" | custom-call | tf_op jit(solution)/shard_map/pallas_call | solution.py:303
  106.0 15.0 %all_to_all.27.got_ref = bf16[8,144,128]{2,1,0:T(8,128)(2,1)S(1)} all-to-all(bf16[8,144,128]{2,1,0:T(8,128)(2,1)S(1)} %get-tuple-element.26), channel_id=1, replica_groups=mesh['sweep'=2,'x'=8,'zh'=4,'zl'=4,'unit'=2] {'x'}, dimensions={0} | all-to-all | bytes 589824 | tf_op jit(solution)/shard_map/all_to_all | solution.py:381
  121.0 1.1 shard_map.68
  122.1 8.2 %all_to_all.28 = f32[4,4,128]{2,1,0:T(4,128)S(1)} all-to-all(f32[4,4,128]{2,1,0:T(4,128)S(1)} %shard_map.68), channel_id=1, replica_groups=mesh['sweep'=2,'x'=8,'zh'=4,'zl'=4,'unit'=2] {'zl'}, dimensions={0} | all-to-all | bytes 16384 | tf_op jit(solution)/shard_map/all_to_all | solution.py:388
  130.4 0.6 copy.8
  (1 shorter events, 0.0 us)
Async XLA Ops:
  1.4 59.0 %all-to-all-start = ((bf16[16,40,128]{2,1,0:T(8,128)(2,1)}), bf16[16,40,128]{2,1,0:T(8,128)(2,1)S(1)}, u32[]{:S(2)}, u32[]{:S(2)}) async-start(bf16[16,40,128]{2,1,0:T(8,128)(2,1)} %shard_map.64), calls=%async_computation | async-start | bytes 327680 | tf_op jit(solution)/shard_map/all_to_all | solution.py:349
  60.5 7.6 %collective-permute-start = (bf16[16,40,128]{2,1,0:T(8,128)(2,1)S(1)}, bf16[16,40,128]{2,1,0:T(8,128)(2,1)S(1)}, u32[]{:S(2)}, u32[]{:S(2)}) collective-permute-start(bf16[16,40,128]{2,1,0:T(8,128)(2,1)S(1)} %all-to-all-done), channel_id=1, source_target_pairs={{0,1},{1,0},{2,3},{3,2},{4,5},{5,4},{6,7},{7,6},{8,9},{9,8},{10,11... | collective-permute-start | bytes 491528 | tf_op jit(solution)/shard_map/ppermute | solution.py:351
  62.4 5.6 %collective-permute-start.1 = (bf16[40,128]{1,0:T(8,128)(2,1)S(1)}, bf16[40,128]{1,0:T(8,128)(2,1)S(1)}, u32[]{:S(2)}, u32[]{:S(2)}) collective-permute-start(bf16[40,128]{1,0:T(8,128)(2,1)S(1)} %slice_bitcast_fusion), channel_id=1, source_target_pairs={{32,0},{64,32},{96,64},{128,96},{160,128},{192,160},{224,192},{33,... | collective-permute-start | bytes 30728 | tf_op jit(solution)/shard_map/ppermute | solution.py:350

commit v4 on v3

--- a/solution.py
+++ b/solution.py
@@ -36,18 +36,19 @@
     return jnp.dot(left, right, preferred_element_type=F32)
 
 
-def gates(rec, proj, prev, guess, ub_ref, cb_ref, par_ref):
+def gates(rec, proj, prev, guess, ub_ref, cb_ref, par_ref, low=0):
     update = jax.nn.sigmoid(proj[0] + rec[:, 0:BLOCK] + ub_ref[...])
     reset = jax.nn.sigmoid(proj[1] + rec[:, BLOCK : 2 * BLOCK])
     inner = rec[:, 2 * BLOCK : 3 * BLOCK] + cb_ref[...]
     cand = jnp.tanh(proj[2] + reset * inner)
     mapped = (1.0 - update) * cand + update * prev
     full = (1.0 - update) * (1.0 - cand * cand) * reset
-    par_ref[0] = update
-    par_ref[1] = (prev - cand) * update * (1.0 - update)
-    par_ref[2] = full * inner * (1.0 - reset)
-    par_ref[3] = full
-    par_ref[4] = mapped - guess
+    high = low + rec.shape[0]
+    par_ref[0, low:high] = update
+    par_ref[1, low:high] = (prev - cand) * update * (1.0 - update)
+    par_ref[2, low:high] = full * inner * (1.0 - reset)
+    par_ref[3, low:high] = full
+    par_ref[4, low:high] = mapped - guess
 
 
 def advance(value, terms, rows):
@@ -66,15 +67,19 @@
     return advance(value, terms, rows) + par_ref[4, low:high, :]
 
 
-def compose_all(par_ref, weight, maps_ref, send_ref, chunks, steps, entry=None):
-    eye = lax.broadcasted_iota(jnp.int32, (BLOCK, BLOCK), 0) == lax.broadcasted_iota(
-        jnp.int32, (BLOCK, BLOCK), 1
-    )
+PART = 4
+
+
+def diagonal_mask():
+    shape = (BLOCK, BLOCK)
+    return lax.broadcasted_iota(jnp.int32, shape, 0) == lax.broadcasted_iota(jnp.int32, shape, 1)
+
+
+def compose_chunks(par_ref, weight, maps_ref, begin, end, chunks, steps):
+    eye = diagonal_mask()
     wide = weight.astype(F32)
-    double = jnp.concatenate([weight, weight], axis=0)
-    part = 4
-    for first in range(0, chunks, part):
-        members = range(first, first + part)
+    for first in range(begin, end, PART):
+        members = range(first, first + PART)
 
         def rows_of(step, c):
             return [par_ref[i, step * chunks + c : step * chunks + c + 1, :] for i in range(4)]
@@ -93,6 +98,11 @@
             ]
         for m, c in zip(current, members):
             maps_ref[c, 0:BLOCK, :] = m
+
+
+def scan_chunks(par_ref, weight, maps_ref, send_ref, chunks, steps, entry=None):
+    eye = diagonal_mask()
+    double = jnp.concatenate([weight, weight], axis=0)
     vector = par_ref[4, 0:chunks, :]
     if entry is not None:
         vector = jnp.concatenate([entry, jnp.zeros((chunks - 1, BLOCK), F32)], axis=0)
@@ -166,8 +176,8 @@
 
 
 def first_maps(
-    index_ref, own_ref, other_ref, next_ref, w_ref, ub_ref, cb_ref,
-    send_ref, maps_ref, par_ref, prev_ref, guess_ref, proj_ref, row_ref,
+    index_ref, own_ref, other_ref, w_ref, ub_ref, cb_ref,
+    maps_ref, par_ref, prev_ref, guess_ref, proj_ref, rec_ref, row_ref,
     *, chunks, steps, blocks, stride,
 ):
     unit, place, group = index_ref[0], index_ref[1], index_ref[2]
@@ -191,7 +201,7 @@
         row = row_ref[pl.ds(side * length + start, 1), :]
         return jnp.broadcast_to(row, (extra, BLOCK))
 
-    row_ref[length - stride : length, :] = next_ref[...].astype(F32)
+    row_ref[length - stride : length, :] = jnp.zeros((stride, BLOCK), F32)
     total = 0.0
     for side, (ref, owner) in enumerate(((own_ref, unit), (other_ref, 1 - unit))):
         row_ref[side * length : side * length + chunks * stride, :] = ref[...].astype(F32)
@@ -217,8 +227,47 @@
     gates(total, proj, prev, guess, ub_ref, cb_ref, par_ref)
     entry = jnp.where(group == 0, par_ref[4, total_steps : total_steps + 1, :], 0.0)
     par_ref[4, total_steps : total_steps + 1, :] = entry
+    rec_ref[...] = total[total_steps - chunks : total_steps]
     here = pl.multiple_of((unit * blocks + place) * BLOCK, BLOCK)
-    compose_all(par_ref, w_ref[pl.ds(here, BLOCK), :], maps_ref, send_ref, chunks, steps, entry)
+    weight = w_ref[pl.ds(here, BLOCK), :]
+    compose_chunks(par_ref, weight, maps_ref, 0, maps_ref.shape[0], chunks, steps)
+
+
+def finish_maps(
+    index_ref, next_ref, rec_ref, w_ref, ub_ref, cb_ref, some_ref, par_in, prev_ref, guess_in, proj_in,
+    send_ref, maps_ref, par_ref, guess_ref, proj_ref, row_ref,
+    *, chunks, steps, blocks,
+):
+    unit, place = index_ref[0], index_ref[1]
+    total_steps = chunks * steps
+    low = total_steps - chunks
+    done = some_ref.shape[0]
+    inputs = (blocks + 1) * steps
+    row_ref[...] = next_ref[...].astype(F32)
+    last = lax.broadcasted_iota(jnp.int32, (chunks, BLOCK), 0) == chunks - 1
+
+    def row(start):
+        return row_ref[pl.ds(start, 1), :]
+
+    par_ref[...] = par_in[...]
+    guess_ref[...] = guess_in[...]
+    proj_ref[...] = proj_in[...]
+    proj = []
+    for g in range(3):
+        proj.append(jnp.where(last, row(inputs + g * steps), proj_in[g, low:total_steps, :]))
+        proj_ref[g, low:total_steps, :] = proj[g]
+    guess = row(place * steps) + row(blocks * steps)
+    guess = jnp.where(last, guess, guess_in[low:total_steps, :])
+    guess_ref[low:total_steps, :] = guess
+    prev = prev_ref[low:total_steps, :]
+    gates(rec_ref[...], proj, prev, guess, ub_ref, cb_ref, par_ref, low)
+    here = pl.multiple_of((unit * blocks + place) * BLOCK, BLOCK)
+    weight = w_ref[pl.ds(here, BLOCK), :]
+    compose_chunks(par_ref, weight, maps_ref, done, chunks, chunks, steps)
+    for c in range(done):
+        maps_ref[c, 0:BLOCK, :] = some_ref[c]
+    entry = par_in[4, total_steps : total_steps + 1, :]
+    scan_chunks(par_ref, weight, maps_ref, send_ref, chunks, steps, entry)
 
 
 def next_maps(
@@ -231,7 +280,9 @@
     total = dot(jnp.concatenate(panels, axis=1), w_ref[...])
     gates(total, proj_ref, prev_ref[...], guess_ref[...], ub_ref, cb_ref, par_ref)
     here = pl.multiple_of((unit * blocks + place) * BLOCK, BLOCK)
-    compose_all(par_ref, w_ref[pl.ds(here, BLOCK), :], maps_ref, send_ref, chunks, steps)
+    weight = w_ref[pl.ds(here, BLOCK), :]
+    compose_chunks(par_ref, weight, maps_ref, 0, chunks, chunks, steps)
+    scan_chunks(par_ref, weight, maps_ref, send_ref, chunks, steps)
 
 
 def solve(index_ref, got_ref, maps_ref, par_ref, w_ref, chunks, steps, blocks, entry=0.0):
@@ -299,7 +350,9 @@
 VMEM = pl.BlockSpec(memory_space=pltpu.VMEM)
 
 
-def call(body, outs, args, scratch=(), first=SMEM, rest=VMEM, limit=24 * 1024 * 1024):
+def call(
+    body, outs, args, scratch=(), first=SMEM, rest=VMEM, limit=24 * 1024 * 1024, cost=None
+):
     return pl.pallas_call(
         body,
         out_shape=[jax.ShapeDtypeStruct(shape, kind) for shape, kind in outs],
@@ -307,6 +360,7 @@
         out_specs=[VMEM] * len(outs),
         scratch_shapes=list(scratch),
         compiler_params=pltpu.CompilerParams(vmem_limit_bytes=limit),
+        cost_estimate=cost,
         interpret=INTERPRET,
     )(*args)
 
@@ -359,12 +413,24 @@
         ((5, total_steps, BLOCK), F32),
     ]
     rows_out = [((total_steps, BLOCK), F32)] * 2
-    first_out = maps_out[:2] + [((5, total_steps + 16, BLOCK), F32)]
-    send, maps, params, prev, guess, proj = call(
+    params_out = [((5, total_steps + 16, BLOCK), F32)]
+    proj_out = [((3, total_steps, BLOCK), F32)]
+    some, params, prev, guess, proj, rec = call(
         functools.partial(first_maps, stride=stride, **sizes),
-        first_out + rows_out + [((3, total_steps, BLOCK), F32)],
-        (index, own, other, after, weight, bias_u, bias_c),
+        [((chunks - PART, BLOCK, BLOCK), F32)]
+        + params_out
+        + rows_out
+        + proj_out
+        + [((chunks, 3 * BLOCK), F32)],
+        (index, own, other, weight, bias_u, bias_c),
         [pltpu.VMEM((sides * (chunks + 1) * stride, BLOCK), F32)],
+        cost=pl.CostEstimate(flops=4 * 10**9, bytes_accessed=4 * 10**6, transcendentals=0),
+    )
+    send, maps, params, guess, proj = call(
+        functools.partial(finish_maps, **sizes),
+        maps_out[:2] + params_out + rows_out[:1] + proj_out,
+        (index, after, rec, weight, bias_u, bias_c, some, params, prev, guess, proj),
+        [pltpu.VMEM((stride, BLOCK), F32)],
     )
     got = lax.all_to_all(send, "x", split_axis=0, concat_axis=0, tiled=True)
     send, prev, guess = call(

time: 131 us -> 130 us (level)
  waiting for transfers between devices: 17.4 us -> 15.2 us
    ppermute x1, waiting for transfers between devices: 4.2 us -> 2.03 us  [shards(): after = lax.ppermute(own[0], 'x', [(k + 1, k) for k in range(groups - 1)])]
    pallas_call x5 -> x6, Pallas kernels: 11.2 us -> 11.9 us  [call(): pl.pallas_call(body, out_shape=[jax.ShapeDtypeStruct(shape, kind) for sha...]
  transfers between devices with their start and end apart: 3 -> 3, of which waited for: 2 -> 2; matrix products, arithmetic and copies ran while one was open for 2% -> 2% of each run, Pallas kernels for 0% -> 2%
where the time goes in v4:
time: 130 us
  blocking collectives  52.6 us (40%)
  starting transfers between devices  46.9 us (36%)
  waiting for transfers between devices  15.2 us (12%)
  Pallas kernels  11.9 us (9%)
  local copies, waits for them, and re-layouts  2.55 us (2%)
    all_to_all x1, starting transfers between devices, shards(): own = lax.all_to_all(payload, Z, split_axis=0, concat_axis=0, tiled=True)  43.7 us
    all_to_all x2, blocking collectives, shards(): got = lax.all_to_all(send, 'x', split_axis=0, concat_axis=0, tiled=True)  34.2 us
    all_to_all x1, waiting for transfers between devices, shards(): own = lax.all_to_all(payload, Z, split_axis=0, concat_axis=0, tiled=True)  13.2 us
    pallas_call x6, Pallas kernels, call(): pl.pallas_call(body, out_shape=[jax.ShapeDtypeStruct(shape, kind) for sha...  11.9 us
    all_to_all x1, blocking collectives, shards(): lax.all_to_all(send, ('zl', 'unit'), split_axis=0, concat_axis=0, tiled=T...  10.2 us
    all_to_all x1, blocking collectives, shards(): final = lax.all_to_all(send, 'zl', split_axis=0, concat_axis=0, tiled=True)  8.23 us
  transfers between devices with their start and end apart: 3, of which 2 were waited for; matrix products, arithmetic and copies ran while one was open for 2% of the time, Pallas kernels for 2%

profile of v4, /device:TPU:80, one launch (start us, length us, event | category | flops | bytes accessed | tf_op | source)
XLA Modules:
  0.0 129.5 jit_solution(1795613998573399949)
XLA Ops:
  0.0 1.4 %shard_map.64 = bf16[16,40,128]{2,1,0:T(8,128)(2,1)} custom-call(f32[4,512]{1,0:T(4,128)} %bitcast.29, bf16[3,4,512]{2,1,0:T(4,128)(2,1)} %bitcast.28, f32[1,512]{1,0:T(1,128)} %start_hbm.1), custom_call_target="tpu_custom_call" | custom-call | tf_op jit(solution)/shard_map/pallas_call | solution.py:356
  1.4 43.7 %all-to-all-start = ((bf16[16,40,128]{2,1,0:T(8,128)(2,1)}), bf16[16,40,128]{2,1,0:T(8,128)(2,1)S(1)}, u32[]{:S(2)}, u32[]{:S(2)}) async-start(bf16[16,40,128]{2,1,0:T(8,128)(2,1)} %shard_map.64), calls=%async_computation | async-start | bytes 327680 | tf_op jit(solution)/shard_map/all_to_all | solution.py:403
  45.1 0.1 pad_add_fusion.index_ref
  45.2 0.8 dynamic-slice_bitcast_fusion.3
  46.0 1.2 dynamic-slice_bitcast_fusion.2
  47.2 0.1 pad_maximum_fusion.w_ref
  47.3 13.2 %all-to-all-done = bf16[16,40,128]{2,1,0:T(8,128)(2,1)S(1)} async-done(((bf16[16,40,128]{2,1,0:T(8,128)(2,1)}), bf16[16,40,128]{2,1,0:T(8,128)(2,1)S(1)}, u32[]{:S(2)}, u32[]{:S(2)}) %all-to-all-start) | async-done | bytes 163872 | tf_op jit(solution)/shard_map/all_to_all | solution.py:403
  60.5 1.9 %collective-permute-start.1 = (bf16[16,40,128]{2,1,0:T(8,128)(2,1)S(1)}, bf16[16,40,128]{2,1,0:T(8,128)(2,1)S(1)}, u32[]{:S(2)}, u32[]{:S(2)}) collective-permute-start(bf16[16,40,128]{2,1,0:T(8,128)(2,1)S(1)} %all-to-all-done), channel_id=1, source_target_pairs={{0,1},{1,0},{2,3},{3,2},{4,5},{5,4},{6,7},{7,6},{8,9},{9,8},{10,11... | collective-permute-start | bytes 491528 | tf_op jit(solution)/shard_map/ppermute | solution.py:405
  62.4 1.3 %collective-permute-start = (bf16[40,128]{1,0:T(8,128)(2,1)S(1)}, bf16[40,128]{1,0:T(8,128)(2,1)S(1)}, u32[]{:S(2)}, u32[]{:S(2)}) collective-permute-start(bf16[40,128]{1,0:T(8,128)(2,1)S(1)} %slice_bitcast_fusion), channel_id=1, source_target_pairs={{32,0},{64,32},{96,64},{128,96},{160,128},{192,160},{224,192},{33,... | collective-permute-start | bytes 30728 | tf_op jit(solution)/shard_map/ppermute | solution.py:404
  63.7 0.0 collective-permute-done.1
  63.8 2.2 %shard_map.65 = (f32[12,128,128]{2,1,0:T(8,128)S(1)}, f32[5,80,128]{2,1,0:T(8,128)S(1)}, f32[64,128]{1,0:T(8,128)S(1)}, f32[64,128]{1,0:T(8,128)S(1)}, f32[3,64,128]{2,1,0:T(8,128)S(1)}, /*index=5*/f32[16,384]{1,0:T(8,128)S(1)}) custom-call(s32[4]{0:T(128)S(1)} %pad_add_fusion.index_ref, bf16[640,128]{1,0:T(8,128)(2,1)S(1)} %bitcast.25, ...), custom_call_target="tpu_custom_call" | custom-call | flops 4000000000 | bytes 4000000 | tf_op jit(solution)/shard_map/pallas_call | solution.py:356
  66.0 2.0 %collective-permute-done.next_ref = bf16[40,128]{1,0:T(8,128)(2,1)S(1)} collective-permute-done((bf16[40,128]{1,0:T(8,128)(2,1)S(1)}, bf16[40,128]{1,0:T(8,128)(2,1)S(1)}, u32[]{:S(2)}, u32[]{:S(2)}) %collective-permute-start) | collective-permute-done | bytes 10272 | tf_op jit(solution)/shard_map/ppermute | solution.py:404
  68.0 2.3 %shard_map.66 = (bf16[8,144,128]{2,1,0:T(8,128)(2,1)S(1)}, f32[16,144,128]{2,1,0:T(8,128)S(1)}, f32[5,80,128]{2,1,0:T(8,128)S(1)}, f32[64,128]{1,0:T(8,128)S(1)}, f32[3,64,128]{2,1,0:T(8,128)S(1)}) custom-call(s32[4]{0:T(128)S(1)} %pad_add_fusion.index_ref, bf16[40,128]{1,0:T(8,128)(2,1)S(1)} %collective-permute-done.next_ref, ...), custom_call_target="tpu_custom_call" | custom-call | tf_op jit(solution)/shard_map/pallas_call | solution.py:356
  70.3 19.2 %all_to_all.25.got_ref = bf16[8,144,128]{2,1,0:T(8,128)(2,1)S(1)} all-to-all(bf16[8,144,128]{2,1,0:T(8,128)(2,1)S(1)} %get-tuple-element.28), channel_id=1, replica_groups=mesh['sweep'=2,'x'=8,'zh'=4,'zl'=4,'unit'=2] {'x'}, dimensions={0} | all-to-all | bytes 589824 | tf_op jit(solution)/shard_map/all_to_all | solution.py:435
  89.6 1.2 shard_map.67
  90.8 10.2 %all_to_all.26.panel_ref = bf16[8,64,128]{2,1,0:T(8,128)(2,1)S(1)} all-to-all(bf16[8,64,128]{2,1,0:T(8,128)(2,1)S(1)} %get-tuple-element.32), channel_id=1, replica_groups=mesh['sweep'=2,'x'=8,'zh'=4,'zl'=4,'unit'=2] {'zl','unit'}, dimensions={0} | all-to-all | bytes 262144 | tf_op jit(solution)/shard_map/all_to_all | solution.py:441
  100.9 3.7 %shard_map.68 = (bf16[8,144,128]{2,1,0:T(8,128)(2,1)S(1)}, f32[16,144,128]{2,1,0:T(8,128)S(1)}, f32[5,64,128]{2,1,0:T(8,128)S(1)}) custom-call(s32[4]{0:T(128)S(1)} %pad_add_fusion.index_ref, bf16[8,64,128]{2,1,0:T(8,128)(2,1)S(1)} %all_to_all.26.panel_ref, f32[3,64,128]{2,1,0:T(8,128)S(1)} %get-tuple-element.33.proj_ref, ...), custom_call_target="tpu_custom_call" | custom-call | tf_op jit(solution)/shard_map/pallas_call | solution.py:356
  104.6 15.0 %all_to_all.27.got_ref = bf16[8,144,128]{2,1,0:T(8,128)(2,1)S(1)} all-to-all(bf16[8,144,128]{2,1,0:T(8,128)(2,1)S(1)} %get-tuple-element.36), channel_id=1, replica_groups=mesh['sweep'=2,'x'=8,'zh'=4,'zl'=4,'unit'=2] {'x'}, dimensions={0} | all-to-all | bytes 589824 | tf_op jit(solution)/shard_map/all_to_all | solution.py:447
  119.6 1.1 shard_map.69
  120.7 8.2 %all_to_all.28 = f32[4,4,128]{2,1,0:T(4,128)S(1)} all-to-all(f32[4,4,128]{2,1,0:T(4,128)S(1)} %shard_map.69), channel_id=1, replica_groups=mesh['sweep'=2,'x'=8,'zh'=4,'zl'=4,'unit'=2] {'zl'}, dimensions={0} | all-to-all | bytes 16384 | tf_op jit(solution)/shard_map/all_to_all | solution.py:454
  128.9 0.6 copy.8
  (1 shorter events, 0.0 us)
Async XLA Ops:
  1.4 59.0 %all-to-all-start = ((bf16[16,40,128]{2,1,0:T(8,128)(2,1)}), bf16[16,40,128]{2,1,0:T(8,128)(2,1)S(1)}, u32[]{:S(2)}, u32[]{:S(2)}) async-start(bf16[16,40,128]{2,1,0:T(8,128)(2,1)} %shard_map.64), calls=%async_computation | async-start | bytes 327680 | tf_op jit(solution)/shard_map/all_to_all | solution.py:403
  60.5 3.3 %collective-permute-start.1 = (bf16[16,40,128]{2,1,0:T(8,128)(2,1)S(1)}, bf16[16,40,128]{2,1,0:T(8,128)(2,1)S(1)}, u32[]{:S(2)}, u32[]{:S(2)}) collective-permute-start(bf16[16,40,128]{2,1,0:T(8,128)(2,1)S(1)} %all-to-all-done), channel_id=1, source_target_pairs={{0,1},{1,0},{2,3},{3,2},{4,5},{5,4},{6,7},{7,6},{8,9},{9,8},{10,11... | collective-permute-start | bytes 491528 | tf_op jit(solution)/shard_map/ppermute | solution.py:405
  62.4 5.6 %collective-permute-start = (bf16[40,128]{1,0:T(8,128)(2,1)S(1)}, bf16[40,128]{1,0:T(8,128)(2,1)S(1)}, u32[]{:S(2)}, u32[]{:S(2)}) collective-permute-start(bf16[40,128]{1,0:T(8,128)(2,1)S(1)} %slice_bitcast_fusion), channel_id=1, source_target_pairs={{32,0},{64,32},{96,64},{128,96},{160,128},{192,160},{224,192},{33,... | collective-permute-start | bytes 30728 | tf_op jit(solution)/shard_map/ppermute | solution.py:404

commit v5 on v4

--- a/solution.py
+++ b/solution.py
@@ -34,6 +34,11 @@
 
 def dot(left, right):
     return jnp.dot(left, right, preferred_element_type=F32)
+
+
+def columns(w_ref, begin, count):
+    begin = pl.multiple_of(begin, BLOCK)
+    return jnp.concatenate([w_ref[g, pl.ds(begin, count), :] for g in range(3)], axis=1)
 
 
 def gates(rec, proj, prev, guess, ub_ref, cb_ref, par_ref, low=0):
@@ -138,17 +143,25 @@
 
 
 def pack(
-    guess_hbm, proj_hbm, start_hbm, send_ref, row_ref, guess_ref, proj_ref, start_ref, sems, *, blocks
-):
+    index_ref, guess_hbm, proj_hbm, start_hbm, w_hbm, ub_hbm, cb_hbm,
+    send_ref, w_ref, ub_ref, cb_ref, row_ref, guess_ref, proj_ref, start_ref, sems, *, blocks,
+):
+    own = pl.ds(pl.multiple_of(index_ref[1] * BLOCK, BLOCK), BLOCK)
+    moves = (
+        (guess_hbm, guess_ref),
+        (proj_hbm, proj_ref),
+        (start_hbm, start_ref),
+        (w_hbm.at[:, :, own], w_ref),
+        (ub_hbm.at[:, own], ub_ref),
+        (cb_hbm.at[:, own], cb_ref),
+    )
     copies = [
         pltpu.make_async_copy(source, target, sems.at[i])
-        for i, (source, target) in enumerate(
-            ((guess_hbm, guess_ref), (proj_hbm, proj_ref), (start_hbm, start_ref))
-        )
+        for i, (source, target) in enumerate(moves)
     ]
     for copy in copies:
         copy.start()
-    for copy in copies:
+    for copy in copies[0:3]:
         copy.wait()
     steps = guess_ref.shape[0]
     high = guess_ref[...].astype(BF16).astype(F32)
@@ -173,6 +186,8 @@
         packed = row_ref[target].astype(BF16)
         for far in range(send_ref.shape[0] // blocks):
             send_ref[far * blocks + target] = packed
+    for copy in copies[3:]:
+        copy.wait()
 
 
 def first_maps(
@@ -209,8 +224,8 @@
             jnp.concatenate(all_steps(side, k * steps) + [one(first + k, side)], axis=0).astype(BF16)
             for k in range(blocks)
         ]
-        columns = w_ref[pl.ds(pl.multiple_of(owner * half, half), half), :]
-        total = total + dot(jnp.concatenate(panels, axis=1), columns)
+        weights = columns(w_ref, owner * half, half)
+        total = total + dot(jnp.concatenate(panels, axis=1), weights)
     proj = []
     for g in range(3):
         start = inputs + g * steps
@@ -228,8 +243,7 @@
     entry = jnp.where(group == 0, par_ref[4, total_steps : total_steps + 1, :], 0.0)
     par_ref[4, total_steps : total_steps + 1, :] = entry
     rec_ref[...] = total[total_steps - chunks : total_steps]
-    here = pl.multiple_of((unit * blocks + place) * BLOCK, BLOCK)
-    weight = w_ref[pl.ds(here, BLOCK), :]
+    weight = columns(w_ref, (unit * blocks + place) * BLOCK, BLOCK)
     compose_chunks(par_ref, weight, maps_ref, 0, maps_ref.shape[0], chunks, steps)
 
 
@@ -261,8 +275,7 @@
     guess_ref[low:total_steps, :] = guess
     prev = prev_ref[low:total_steps, :]
     gates(rec_ref[...], proj, prev, guess, ub_ref, cb_ref, par_ref, low)
-    here = pl.multiple_of((unit * blocks + place) * BLOCK, BLOCK)
-    weight = w_ref[pl.ds(here, BLOCK), :]
+    weight = columns(w_ref, (unit * blocks + place) * BLOCK, BLOCK)
     compose_chunks(par_ref, weight, maps_ref, done, chunks, chunks, steps)
     for c in range(done):
         maps_ref[c, 0:BLOCK, :] = some_ref[c]
@@ -277,10 +290,9 @@
     unit, place = index_ref[0], index_ref[1]
     sides = panel_ref.shape[0] // blocks
     panels = [panel_ref[k * sides + side] for side in range(sides) for k in range(blocks)]
-    total = dot(jnp.concatenate(panels, axis=1), w_ref[...])
+    total = dot(jnp.concatenate(panels, axis=1), columns(w_ref, 0, w_ref.shape[1]))
     gates(total, proj_ref, prev_ref[...], guess_ref[...], ub_ref, cb_ref, par_ref)
-    here = pl.multiple_of((unit * blocks + place) * BLOCK, BLOCK)
-    weight = w_ref[pl.ds(here, BLOCK), :]
+    weight = columns(w_ref, (unit * blocks + place) * BLOCK, BLOCK)
     compose_chunks(par_ref, weight, maps_ref, 0, chunks, chunks, steps)
     scan_chunks(par_ref, weight, maps_ref, send_ref, chunks, steps)
 
@@ -306,8 +318,7 @@
         through = jnp.sum(column * maps_ref[c, 0:BLOCK, :], axis=0, keepdims=True)
         entries.append(through + maps_ref[c, BLOCK : BLOCK + 1, :])
     entries = jnp.concatenate(entries, axis=0)
-    here = pl.multiple_of((unit * blocks + place) * BLOCK, BLOCK)
-    weight = w_ref[pl.ds(here, BLOCK), :]
+    weight = columns(w_ref, (unit * blocks + place) * BLOCK, BLOCK)
     double = jnp.concatenate([weight, weight], axis=0)
     current, after = entries, []
     for step in range(steps):
@@ -379,26 +390,35 @@
     group = lax.axis_index("x")
     index = jnp.stack([unit, place, group, lax.axis_index("zh")]).astype(jnp.int32)
 
-    weight = lax.dynamic_slice_in_dim(recurrent, place * BLOCK, BLOCK, 2)
-    weight = jnp.concatenate([weight[:, g, :] for g in range(3)], axis=1)
-    bias_u = lax.dynamic_slice_in_dim(update_bias, place * BLOCK, BLOCK, 0)[None]
-    bias_c = lax.dynamic_slice_in_dim(candidate_bias, place * BLOCK, BLOCK, 0)[None]
     stride = -(-((blocks + 1) * (steps + 1) + 3 * steps) // 8) * 8
-    here = pl.BlockSpec(memory_space=pl.ANY)
-    (payload,) = call(
+    far = [
+        pltpu.with_memory_space_constraint(value, pltpu.HBM)
+        for value in (
+            initial_guess[0],
+            jnp.transpose(projections[0], (1, 0, 2)),
+            start_state,
+            jnp.transpose(recurrent, (1, 0, 2)),
+            update_bias[None],
+            candidate_bias[None],
+        )
+    ]
+    payload, weight, bias_u, bias_c = call(
         functools.partial(pack, blocks=blocks),
-        [((chunks, stride, BLOCK), BF16)],
-        (initial_guess[0], jnp.transpose(projections[0], (1, 0, 2)), start_state),
+        [
+            ((chunks, stride, BLOCK), BF16),
+            ((3, full_width, BLOCK), BF16),
+            ((1, BLOCK), F32),
+            ((1, BLOCK), F32),
+        ],
+        (index, *far),
         [
             pltpu.VMEM((blocks, stride, BLOCK), F32),
             pltpu.VMEM((steps, width_dev), F32),
             pltpu.VMEM((3, steps, width_dev), BF16),
             pltpu.VMEM((1, width_dev), F32),
-            pltpu.SemaphoreType.DMA((3,)),
+            pltpu.SemaphoreType.DMA((len(far),)),
         ],
-        here,
-        here,
-        60 * 1024 * 1024,
+        rest=pl.BlockSpec(memory_space=pltpu.HBM),
     )
     own = lax.all_to_all(payload, Z, split_axis=0, concat_axis=0, tiled=True)
     after = lax.ppermute(own[0], "x", [(k + 1, k) for k in range(groups - 1)])

time: 130 us -> 130 us (level)
  blocking collectives: 52.6 us -> 111 us
  starting transfers between devices: 46.9 us -> 3.25 us
  waiting for transfers between devices: 15.2 us -> 2.06 us
  local copies, waits for them, and re-layouts: 2.55 us -> 0.6 us
    all_to_all x0 -> x1, blocking collectives: none -> 58.8 us  [shards(): own = lax.all_to_all(payload, Z, split_axis=0, concat_axis=0, tiled=True)]
    all_to_all x1 -> x0, starting transfers between devices: 43.7 us -> none  [shards(): own = lax.all_to_all(payload, Z, split_axis=0, concat_axis=0, tiled=True)]
    all_to_all x1 -> x0, waiting for transfers between devices: 13.2 us -> none  [shards(): own = lax.all_to_all(payload, Z, split_axis=0, concat_axis=0, tiled=True)]
  transfers between devices with their start and end apart: 3 -> 2, of which waited for: 2 -> 1; matrix products, arithmetic and copies ran while one was open for 2% -> 0% of each run, Pallas kernels for 2% -> 2%
where the time goes in v5:
time: 130 us
  blocking collectives  111 us (85%)
  Pallas kernels  12.3 us (9%)
  starting transfers between devices  3.25 us (2%)
  waiting for transfers between devices  2.06 us (2%)
    all_to_all x1, blocking collectives, shards(): own = lax.all_to_all(payload, Z, split_axis=0, concat_axis=0, tiled=True)  58.8 us
    all_to_all x2, blocking collectives, shards(): got = lax.all_to_all(send, 'x', split_axis=0, concat_axis=0, tiled=True)  34.2 us
    pallas_call x6, Pallas kernels, call(): pl.pallas_call(body, out_shape=[jax.ShapeDtypeStruct(shape, kind) for sha...  12.3 us
    all_to_all x1, blocking collectives, shards(): lax.all_to_all(send, ('zl', 'unit'), split_axis=0, concat_axis=0, tiled=T...  10.2 us
    all_to_all x1, blocking collectives, shards(): final = lax.all_to_all(send, 'zl', split_axis=0, concat_axis=0, tiled=True)  8.22 us
  transfers between devices with their start and end apart: 2, of which 1 were waited for; matrix products, arithmetic and copies ran while one was open for 0% of the time, Pallas kernels for 2%

profile of v5, /device:TPU:80, one launch (start us, length us, event | category | flops | bytes accessed | tf_op | source)
XLA Modules:
  0.0 129.7 jit_solution(1550854423333076251)
XLA Ops:
  0.0 0.1 pad_add_fusion.index_ref
  0.1 1.8 %shard_map.64 = (bf16[16,40,128]{2,1,0:T(8,128)(2,1)S(1)}, bf16[3,1024,128]{2,1,0:T(8,128)(2,1)S(1)}, f32[1,128]{1,0:T(1,128)S(1)}, f32[1,128]{1,0:T(1,128)S(1)}) custom-call(s32[4]{0:T(128)S(1)} %pad_add_fusion.index_ref, f32[4,512]{1,0:T(4,128)} %bitcast.23, bf16[3,4,512]{2,1,0:T(4,128)(2,1)} %bitcast.22, f32[1,512]{1,0:T(1,128)} %start_hbm.1, ...), custom_call_target="tpu_custom_call" | custom-call | tf_op jit(solution)/shard_map/pallas_call | solution.py:367
  1.9 58.8 %all_to_all.25 = bf16[16,40,128]{2,1,0:T(8,128)(2,1)S(1)} all-to-all(bf16[16,40,128]{2,1,0:T(8,128)(2,1)S(1)} %get-tuple-element.26), channel_id=1, replica_groups=mesh['sweep'=2,'x'=8,'zh'=4,'zl'=4,'unit'=2] {'zh','zl'}, dimensions={0} | all-to-all | bytes 327680 | tf_op jit(solution)/shard_map/all_to_all | solution.py:423
  60.7 1.9 %collective-permute-start.1 = (bf16[16,40,128]{2,1,0:T(8,128)(2,1)S(1)}, bf16[16,40,128]{2,1,0:T(8,128)(2,1)S(1)}, u32[]{:S(2)}, u32[]{:S(2)}) collective-permute-start(bf16[16,40,128]{2,1,0:T(8,128)(2,1)S(1)} %all_to_all.25), channel_id=1, source_target_pairs={{0,1},{1,0},{2,3},{3,2},{4,5},{5,4},{6,7},{7,6},{8,9},{9,8},{10,11... | collective-permute-start | bytes 491528 | tf_op jit(solution)/shard_map/ppermute | solution.py:425
  62.6 1.3 %collective-permute-start = (bf16[40,128]{1,0:T(8,128)(2,1)S(1)}, bf16[40,128]{1,0:T(8,128)(2,1)S(1)}, u32[]{:S(2)}, u32[]{:S(2)}) collective-permute-start(bf16[40,128]{1,0:T(8,128)(2,1)S(1)} %slice_bitcast_fusion), channel_id=1, source_target_pairs={{32,0},{64,32},{96,64},{128,96},{160,128},{192,160},{224,192},{33,... | collective-permute-start | bytes 30728 | tf_op jit(solution)/shard_map/ppermute | solution.py:424
  63.9 0.0 collective-permute-done.1
  64.0 2.2 %shard_map.65 = (f32[12,128,128]{2,1,0:T(8,128)S(1)}, f32[5,80,128]{2,1,0:T(8,128)S(1)}, f32[64,128]{1,0:T(8,128)S(1)}, f32[64,128]{1,0:T(8,128)S(1)}, f32[3,64,128]{2,1,0:T(8,128)S(1)}, /*index=5*/f32[16,384]{1,0:T(8,128)S(1)}) custom-call(s32[4]{0:T(128)S(1)} %pad_add_fusion.index_ref, bf16[640,128]{1,0:T(8,128)(2,1)S(1)} %bitcast.18, ...), custom_call_target="tpu_custom_call" | custom-call | flops 4000000000 | bytes 4000000 | tf_op jit(solution)/shard_map/pallas_call | solution.py:367
  66.2 2.0 %collective-permute-done.next_ref = bf16[40,128]{1,0:T(8,128)(2,1)S(1)} collective-permute-done((bf16[40,128]{1,0:T(8,128)(2,1)S(1)}, bf16[40,128]{1,0:T(8,128)(2,1)S(1)}, u32[]{:S(2)}, u32[]{:S(2)}) %collective-permute-start) | collective-permute-done | bytes 10272 | tf_op jit(solution)/shard_map/ppermute | solution.py:424
  68.2 2.3 %shard_map.66 = (bf16[8,144,128]{2,1,0:T(8,128)(2,1)S(1)}, f32[16,144,128]{2,1,0:T(8,128)S(1)}, f32[5,80,128]{2,1,0:T(8,128)S(1)}, f32[64,128]{1,0:T(8,128)S(1)}, f32[3,64,128]{2,1,0:T(8,128)S(1)}) custom-call(s32[4]{0:T(128)S(1)} %pad_add_fusion.index_ref, bf16[40,128]{1,0:T(8,128)(2,1)S(1)} %collective-permute-done.next_ref, ...), custom_call_target="tpu_custom_call" | custom-call | tf_op jit(solution)/shard_map/pallas_call | solution.py:367
  70.5 19.2 %all_to_all.26.got_ref = bf16[8,144,128]{2,1,0:T(8,128)(2,1)S(1)} all-to-all(bf16[8,144,128]{2,1,0:T(8,128)(2,1)S(1)} %get-tuple-element.36), channel_id=1, replica_groups=mesh['sweep'=2,'x'=8,'zh'=4,'zl'=4,'unit'=2] {'x'}, dimensions={0} | all-to-all | bytes 589824 | tf_op jit(solution)/shard_map/all_to_all | solution.py:455
  89.8 1.2 shard_map.67
  91.0 10.2 %all_to_all.27.panel_ref = bf16[8,64,128]{2,1,0:T(8,128)(2,1)S(1)} all-to-all(bf16[8,64,128]{2,1,0:T(8,128)(2,1)S(1)} %get-tuple-element.40), channel_id=1, replica_groups=mesh['sweep'=2,'x'=8,'zh'=4,'zl'=4,'unit'=2] {'zl','unit'}, dimensions={0} | all-to-all | bytes 262144 | tf_op jit(solution)/shard_map/all_to_all | solution.py:461
  101.1 3.7 %shard_map.68 = (bf16[8,144,128]{2,1,0:T(8,128)(2,1)S(1)}, f32[16,144,128]{2,1,0:T(8,128)S(1)}, f32[5,64,128]{2,1,0:T(8,128)S(1)}) custom-call(s32[4]{0:T(128)S(1)} %pad_add_fusion.index_ref, bf16[8,64,128]{2,1,0:T(8,128)(2,1)S(1)} %all_to_all.27.panel_ref, f32[3,64,128]{2,1,0:T(8,128)S(1)} %get-tuple-element.41.proj_ref, ...), custom_call_target="tpu_custom_call" | custom-call | tf_op jit(solution)/shard_map/pallas_call | solution.py:367
  104.8 15.0 %all_to_all.28.got_ref = bf16[8,144,128]{2,1,0:T(8,128)(2,1)S(1)} all-to-all(bf16[8,144,128]{2,1,0:T(8,128)(2,1)S(1)} %get-tuple-element.44), channel_id=1, replica_groups=mesh['sweep'=2,'x'=8,'zh'=4,'zl'=4,'unit'=2] {'x'}, dimensions={0} | all-to-all | bytes 589824 | tf_op jit(solution)/shard_map/all_to_all | solution.py:467
  119.8 1.1 shard_map.69
  120.9 8.2 %all_to_all.29 = f32[4,4,128]{2,1,0:T(4,128)S(1)} all-to-all(f32[4,4,128]{2,1,0:T(4,128)S(1)} %shard_map.69), channel_id=1, replica_groups=mesh['sweep'=2,'x'=8,'zh'=4,'zl'=4,'unit'=2] {'zl'}, dimensions={0} | all-to-all | bytes 16384 | tf_op jit(solution)/shard_map/all_to_all | solution.py:474
  129.1 0.6 copy.8
  (1 shorter events, 0.0 us)
Async XLA Ops:
  60.7 3.3 %collective-permute-start.1 = (bf16[16,40,128]{2,1,0:T(8,128)(2,1)S(1)}, bf16[16,40,128]{2,1,0:T(8,128)(2,1)S(1)}, u32[]{:S(2)}, u32[]{:S(2)}) collective-permute-start(bf16[16,40,128]{2,1,0:T(8,128)(2,1)S(1)} %all_to_all.25), channel_id=1, source_target_pairs={{0,1},{1,0},{2,3},{3,2},{4,5},{5,4},{6,7},{7,6},{8,9},{9,8},{10,11... | collective-permute-start | bytes 491528 | tf_op jit(solution)/shard_map/ppermute | solution.py:425
  62.6 5.6 %collective-permute-start = (bf16[40,128]{1,0:T(8,128)(2,1)S(1)}, bf16[40,128]{1,0:T(8,128)(2,1)S(1)}, u32[]{:S(2)}, u32[]{:S(2)}) collective-permute-start(bf16[40,128]{1,0:T(8,128)(2,1)S(1)} %slice_bitcast_fusion), channel_id=1, source_target_pairs={{32,0},{64,32},{96,64},{128,96},{160,128},{192,160},{224,192},{33,... | collective-permute-start | bytes 30728 | tf_op jit(solution)/shard_map/ppermute | solution.py:424

commit v6 on v5

--- a/solution.py
+++ b/solution.py
@@ -14,6 +14,7 @@
 Z = ("zh", "zl")
 INTERPRET = False
 ROWS = BLOCK + 16
+SENT = BLOCK + 8
 F32 = jnp.float32
 BF16 = jnp.bfloat16
 
@@ -105,8 +106,7 @@
             maps_ref[c, 0:BLOCK, :] = m
 
 
-def scan_chunks(par_ref, weight, maps_ref, send_ref, chunks, steps, entry=None):
-    eye = diagonal_mask()
+def add_vectors(par_ref, weight, maps_ref, begin, end, chunks, steps, entry=None):
     double = jnp.concatenate([weight, weight], axis=0)
     vector = par_ref[4, 0:chunks, :]
     if entry is not None:
@@ -115,11 +115,13 @@
     for step in range(1, steps):
         vector = advance_rows(vector, double, par_ref, step * chunks, (step + 1) * chunks)
     pad = jnp.zeros((ROWS - BLOCK - 1, BLOCK), F32)
-    for c in range(chunks):
+    for c in range(begin, end):
         maps_ref[c, BLOCK:ROWS, :] = jnp.concatenate([vector[c : c + 1], pad], axis=0)
-    width = 1
-    while width < chunks:
-        for left in range(width - 1, chunks, 2 * width):
+
+
+def scan(maps_ref, begin, end, width, limit):
+    while width < limit:
+        for left in range(begin + width - 1, end, 2 * width):
             before = jnp.concatenate(split2(maps_ref[left]), axis=1)
             for right in range(left + 1, left + 1 + width):
                 high, low = split2(maps_ref[right, 0:BLOCK, :])
@@ -130,16 +132,20 @@
                 maps_ref[right, 0:BLOCK, :] = both[0:BLOCK]
                 maps_ref[right, BLOCK:ROWS, :] = both[BLOCK:] + maps_ref[right, BLOCK:ROWS, :]
         width *= 2
+
+
+def send_map(maps_ref, send_ref, chunks):
+    eye = diagonal_mask()
     matrix = maps_ref[chunks - 1, 0:BLOCK, :]
     diagonal = jnp.sum(jnp.where(eye, matrix, 0.0), axis=0, keepdims=True)
     tail = [p.astype(F32) for p in split3(diagonal)]
     tail += [p.astype(F32) for p in split3(maps_ref[chunks - 1, BLOCK : BLOCK + 1, :])]
-    tail.append(jnp.zeros((ROWS - BLOCK - 6, BLOCK), F32))
+    tail.append(jnp.zeros((SENT - BLOCK - 6, BLOCK), F32))
     matrix = jnp.where(eye, 0.0, matrix).astype(BF16)
     tail = jnp.concatenate(tail, axis=0).astype(BF16)
     for peer in range(send_ref.shape[0]):
         send_ref[peer, 0:BLOCK, :] = matrix
-        send_ref[peer, BLOCK:ROWS, :] = tail
+        send_ref[peer, BLOCK:SENT, :] = tail
 
 
 def pack(
@@ -244,7 +250,10 @@
     par_ref[4, total_steps : total_steps + 1, :] = entry
     rec_ref[...] = total[total_steps - chunks : total_steps]
     weight = columns(w_ref, (unit * blocks + place) * BLOCK, BLOCK)
-    compose_chunks(par_ref, weight, maps_ref, 0, maps_ref.shape[0], chunks, steps)
+    done = maps_ref.shape[0]
+    compose_chunks(par_ref, weight, maps_ref, 0, done, chunks, steps)
+    add_vectors(par_ref, weight, maps_ref, 0, done, chunks, steps, entry)
+    scan(maps_ref, 0, done, 1, PART)
 
 
 def finish_maps(
@@ -278,9 +287,11 @@
     weight = columns(w_ref, (unit * blocks + place) * BLOCK, BLOCK)
     compose_chunks(par_ref, weight, maps_ref, done, chunks, chunks, steps)
     for c in range(done):
-        maps_ref[c, 0:BLOCK, :] = some_ref[c]
-    entry = par_in[4, total_steps : total_steps + 1, :]
-    scan_chunks(par_ref, weight, maps_ref, send_ref, chunks, steps, entry)
+        maps_ref[c] = some_ref[c]
+    add_vectors(par_ref, weight, maps_ref, done, chunks, chunks, steps)
+    scan(maps_ref, done, chunks, 1, PART)
+    scan(maps_ref, 0, chunks, PART, chunks)
+    send_map(maps_ref, send_ref, chunks)
 
 
 def next_maps(
@@ -294,7 +305,9 @@
     gates(total, proj_ref, prev_ref[...], guess_ref[...], ub_ref, cb_ref, par_ref)
     weight = columns(w_ref, (unit * blocks + place) * BLOCK, BLOCK)
     compose_chunks(par_ref, weight, maps_ref, 0, chunks, chunks, steps)
-    scan_chunks(par_ref, weight, maps_ref, send_ref, chunks, steps)
+    add_vectors(par_ref, weight, maps_ref, 0, chunks, chunks, steps)
+    scan(maps_ref, 0, chunks, 1, chunks)
+    send_map(maps_ref, send_ref, chunks)
 
 
 def solve(index_ref, got_ref, maps_ref, par_ref, w_ref, chunks, steps, blocks, entry=0.0):
@@ -303,7 +316,7 @@
     def pass_group(k, delta):
         block = got_ref[k]
         matrix = block[0:BLOCK]
-        tail = block[BLOCK:ROWS].astype(F32)
+        tail = block[BLOCK:SENT].astype(F32)
         diagonal = tail[0:1] + tail[1:2] + tail[2:3]
         vector = tail[3:4] + tail[4:5] + tail[5:6]
         terms = dot(
@@ -311,7 +324,9 @@
         )
         return terms + delta * diagonal + vector
 
-    delta = lax.fori_loop(0, group, pass_group, jnp.zeros((16, BLOCK), F32))
+    tail = got_ref[0][BLOCK:SENT].astype(F32)
+    begin = jnp.where(group > 0, tail[3:4] + tail[4:5] + tail[5:6], 0.0)
+    delta = lax.fori_loop(1, group, pass_group, jnp.broadcast_to(begin, (16, BLOCK)))
     column = jnp.transpose(jnp.broadcast_to(delta[0:1], (BLOCK, BLOCK)))
     entries = [delta[0:1] + entry]
     for c in range(chunks - 1):
@@ -428,7 +443,7 @@
 
     sizes = dict(chunks=chunks, steps=steps, blocks=blocks)
     maps_out = [
-        ((groups, ROWS, BLOCK), BF16),
+        ((groups, SENT, BLOCK), BF16),
         ((chunks, ROWS, BLOCK), F32),
         ((5, total_steps, BLOCK), F32),
     ]
@@ -437,7 +452,7 @@
     proj_out = [((3, total_steps, BLOCK), F32)]
     some, params, prev, guess, proj, rec = call(
         functools.partial(first_maps, stride=stride, **sizes),
-        [((chunks - PART, BLOCK, BLOCK), F32)]
+        [((chunks - PART, ROWS, BLOCK), F32)]
         + params_out
         + rows_out
         + proj_out

time: 130 us -> 130 us (level)
  no operation moved by 1% of the time
where the time goes in v6:
time: 130 us
  blocking collectives  111 us (85%)
  Pallas kernels  12.7 us (10%)
  starting transfers between devices  3.25 us (2%)
    all_to_all x1, blocking collectives, shards(): own = lax.all_to_all(payload, Z, split_axis=0, concat_axis=0, tiled=True)  58.8 us
    all_to_all x2, blocking collectives, shards(): got = lax.all_to_all(send, 'x', split_axis=0, concat_axis=0, tiled=True)  34.3 us
    pallas_call x6, Pallas kernels, call(): pl.pallas_call(body, out_shape=[jax.ShapeDtypeStruct(shape, kind) for sha...  12.7 us
    all_to_all x1, blocking collectives, shards(): lax.all_to_all(send, ('zl', 'unit'), split_axis=0, concat_axis=0, tiled=T...  10.2 us
    all_to_all x1, blocking collectives, shards(): final = lax.all_to_all(send, 'zl', split_axis=0, concat_axis=0, tiled=True)  8.24 us
  transfers between devices with their start and end apart: 2, of which 1 were waited for; matrix products, arithmetic and copies ran while one was open for 0% of the time, Pallas kernels for 2%

profile of v6, /device:TPU:80, one launch (start us, length us, event | category | flops | bytes accessed | tf_op | source)
XLA Modules:
  0.0 129.5 jit_solution(8601664318771072433)
XLA Ops:
  0.0 0.1 pad_add_fusion.index_ref
  0.1 1.8 %shard_map.64 = (bf16[16,40,128]{2,1,0:T(8,128)(2,1)S(1)}, bf16[3,1024,128]{2,1,0:T(8,128)(2,1)S(1)}, f32[1,128]{1,0:T(1,128)S(1)}, f32[1,128]{1,0:T(1,128)S(1)}) custom-call(s32[4]{0:T(128)S(1)} %pad_add_fusion.index_ref, f32[4,512]{1,0:T(4,128)} %bitcast.23, bf16[3,4,512]{2,1,0:T(4,128)(2,1)} %bitcast.22, f32[1,512]{1,0:T(1,128)} %start_hbm.1, ...), custom_call_target="tpu_custom_call" | custom-call | tf_op jit(solution)/shard_map/pallas_call | solution.py:382
  1.9 58.8 %all_to_all.25 = bf16[16,40,128]{2,1,0:T(8,128)(2,1)S(1)} all-to-all(bf16[16,40,128]{2,1,0:T(8,128)(2,1)S(1)} %get-tuple-element.26), channel_id=1, replica_groups=mesh['sweep'=2,'x'=8,'zh'=4,'zl'=4,'unit'=2] {'zh','zl'}, dimensions={0} | all-to-all | bytes 327680 | tf_op jit(solution)/shard_map/all_to_all | solution.py:438
  60.7 1.9 %collective-permute-start.1 = (bf16[16,40,128]{2,1,0:T(8,128)(2,1)S(1)}, bf16[16,40,128]{2,1,0:T(8,128)(2,1)S(1)}, u32[]{:S(2)}, u32[]{:S(2)}) collective-permute-start(bf16[16,40,128]{2,1,0:T(8,128)(2,1)S(1)} %all_to_all.25), channel_id=1, source_target_pairs={{0,1},{1,0},{2,3},{3,2},{4,5},{5,4},{6,7},{7,6},{8,9},{9,8},{10,11... | collective-permute-start | bytes 491528 | tf_op jit(solution)/shard_map/ppermute | solution.py:440
  62.6 1.3 %collective-permute-start = (bf16[40,128]{1,0:T(8,128)(2,1)S(1)}, bf16[40,128]{1,0:T(8,128)(2,1)S(1)}, u32[]{:S(2)}, u32[]{:S(2)}) collective-permute-start(bf16[40,128]{1,0:T(8,128)(2,1)S(1)} %slice_bitcast_fusion), channel_id=1, source_target_pairs={{32,0},{64,32},{96,64},{128,96},{160,128},{192,160},{224,192},{33,... | collective-permute-start | bytes 30728 | tf_op jit(solution)/shard_map/ppermute | solution.py:439
  63.9 0.0 collective-permute-done.1
  64.0 3.0 %shard_map.65 = (f32[12,144,128]{2,1,0:T(8,128)S(1)}, f32[5,80,128]{2,1,0:T(8,128)S(1)}, f32[64,128]{1,0:T(8,128)S(1)}, f32[64,128]{1,0:T(8,128)S(1)}, f32[3,64,128]{2,1,0:T(8,128)S(1)}, /*index=5*/f32[16,384]{1,0:T(8,128)S(1)}) custom-call(s32[4]{0:T(128)S(1)} %pad_add_fusion.index_ref, bf16[640,128]{1,0:T(8,128)(2,1)S(1)} %bitcast.18, ...), custom_call_target="tpu_custom_call" | custom-call | flops 4000000000 | bytes 4000000 | tf_op jit(solution)/shard_map/pallas_call | solution.py:382
  67.0 1.3 collective-permute-done.next_ref
  68.2 2.0 %shard_map.66 = (bf16[8,136,128]{2,1,0:T(8,128)(2,1)S(1)}, f32[16,144,128]{2,1,0:T(8,128)S(1)}, f32[5,80,128]{2,1,0:T(8,128)S(1)}, f32[64,128]{1,0:T(8,128)S(1)}, f32[3,64,128]{2,1,0:T(8,128)S(1)}) custom-call(s32[4]{0:T(128)S(1)} %pad_add_fusion.index_ref, bf16[40,128]{1,0:T(8,128)(2,1)S(1)} %collective-permute-done.next_ref, ...), custom_call_target="tpu_custom_call" | custom-call | tf_op jit(solution)/shard_map/pallas_call | solution.py:382
  70.2 19.7 %all_to_all.26.got_ref = bf16[8,136,128]{2,1,0:T(8,128)(2,1)S(1)} all-to-all(bf16[8,136,128]{2,1,0:T(8,128)(2,1)S(1)} %get-tuple-element.36), channel_id=1, replica_groups=mesh['sweep'=2,'x'=8,'zh'=4,'zl'=4,'unit'=2] {'x'}, dimensions={0} | all-to-all | bytes 557056 | tf_op jit(solution)/shard_map/all_to_all | solution.py:470
  89.9 1.2 shard_map.67
  91.1 10.2 %all_to_all.27.panel_ref = bf16[8,64,128]{2,1,0:T(8,128)(2,1)S(1)} all-to-all(bf16[8,64,128]{2,1,0:T(8,128)(2,1)S(1)} %get-tuple-element.40), channel_id=1, replica_groups=mesh['sweep'=2,'x'=8,'zh'=4,'zl'=4,'unit'=2] {'zl','unit'}, dimensions={0} | all-to-all | bytes 262144 | tf_op jit(solution)/shard_map/all_to_all | solution.py:476
  101.2 3.7 %shard_map.68 = (bf16[8,136,128]{2,1,0:T(8,128)(2,1)S(1)}, f32[16,144,128]{2,1,0:T(8,128)S(1)}, f32[5,64,128]{2,1,0:T(8,128)S(1)}) custom-call(s32[4]{0:T(128)S(1)} %pad_add_fusion.index_ref, bf16[8,64,128]{2,1,0:T(8,128)(2,1)S(1)} %all_to_all.27.panel_ref, f32[3,64,128]{2,1,0:T(8,128)S(1)} %get-tuple-element.41.proj_ref, ...), custom_call_target="tpu_custom_call" | custom-call | tf_op jit(solution)/shard_map/pallas_call | solution.py:382
  104.9 14.7 %all_to_all.28.got_ref = bf16[8,136,128]{2,1,0:T(8,128)(2,1)S(1)} all-to-all(bf16[8,136,128]{2,1,0:T(8,128)(2,1)S(1)} %get-tuple-element.44), channel_id=1, replica_groups=mesh['sweep'=2,'x'=8,'zh'=4,'zl'=4,'unit'=2] {'x'}, dimensions={0} | all-to-all | bytes 557056 | tf_op jit(solution)/shard_map/all_to_all | solution.py:482
  119.6 1.1 shard_map.69
  120.7 8.2 %all_to_all.29 = f32[4,4,128]{2,1,0:T(4,128)S(1)} all-to-all(f32[4,4,128]{2,1,0:T(4,128)S(1)} %shard_map.69), channel_id=1, replica_groups=mesh['sweep'=2,'x'=8,'zh'=4,'zl'=4,'unit'=2] {'zl'}, dimensions={0} | all-to-all | bytes 16384 | tf_op jit(solution)/shard_map/all_to_all | solution.py:489
  128.9 0.6 copy.8
  (1 shorter events, 0.0 us)
Async XLA Ops:
  60.7 3.3 %collective-permute-start.1 = (bf16[16,40,128]{2,1,0:T(8,128)(2,1)S(1)}, bf16[16,40,128]{2,1,0:T(8,128)(2,1)S(1)}, u32[]{:S(2)}, u32[]{:S(2)}) collective-permute-start(bf16[16,40,128]{2,1,0:T(8,128)(2,1)S(1)} %all_to_all.25), channel_id=1, source_target_pairs={{0,1},{1,0},{2,3},{3,2},{4,5},{5,4},{6,7},{7,6},{8,9},{9,8},{10,11... | collective-permute-start | bytes 491528 | tf_op jit(solution)/shard_map/ppermute | solution.py:440
  62.6 5.6 %collective-permute-start = (bf16[40,128]{1,0:T(8,128)(2,1)S(1)}, bf16[40,128]{1,0:T(8,128)(2,1)S(1)}, u32[]{:S(2)}, u32[]{:S(2)}) collective-permute-start(bf16[40,128]{1,0:T(8,128)(2,1)S(1)} %slice_bitcast_fusion), channel_id=1, source_target_pairs={{32,0},{64,32},{96,64},{128,96},{160,128},{192,160},{224,192},{33,... | collective-permute-start | bytes 30728 | tf_op jit(solution)/shard_map/ppermute | solution.py:439
